TPU v7x, 256 devices: a whole 4x4x8 slice. The times are simulated.
256 devices in a mesh: ep: 32 (over z_lo, y, x), dp: 8 (over z_hi, core).
Axes of the slice: x: 4, y: 4, z: 8 (z_hi: 4, z_lo: 2; z = z_hi * 2 + z_lo), core: 2. Of those that a mesh axis runs over, the one named last changes fastest.
Arguments:
- tokens: bfloat16 [16384, 2048], P(('dp', 'ep')), parts along dimension 0, may hold values from -6 to 6
- expert_ids: int32 [16384, 8], P(('dp', 'ep')), parts along dimension 0, may hold values from 0 to 31, all different within a row; in each aligned block of 64 rows (0 to 63, 64 to 127, ...) at most 32 rows name the same one
- gate_probs: float32 [16384, 8], P(('dp', 'ep')), parts along dimension 0, may hold values from 0.05 to 1
- w_gate: bfloat16 [32, 2048, 768], P('ep'), may hold values from -0.125 to 0.125
- w_up: bfloat16 [32, 2048, 768], P('ep'), may hold values from -0.125 to 0.125
- w_down: bfloat16 [32, 768, 2048], P('ep'), may hold values from -0.21875 to 0.21875
Outputs:
- combined: bfloat16 [16384, 2048], P(('dp', 'ep')), parts along dimension 0
There are 8 independent parts, one for each index of `dp`. A program takes and returns all parts, laid end to end along the dimension named above; an argument that names none is the same for every part. Nothing has to cross between parts.
Inputs may be any that keep to these rules, and one draw needn't show every extreme that they name: `expert_ids`: each row names 8 different experts. Among the rows of one index of ep (aligned blocks of 64 rows) no expert is named by more than 32 rows, and in every draw some expert is named by exactly 32 rows of some block. Expert popularity is skewed.
All inputs are finite; a program needn't handle non-finite values.
Results may differ from a plain program's by a relative error of at most 0.0085.
Values may be sent and summed in bfloat16 or wider, within the bound.
A program may use at most 64 MiB of HBM per device.

v0:
```python
import jax
import jax.numpy as jnp
from jax import lax
from jax.sharding import PartitionSpec as P


def expert_ffn(row_block, gate_matrix, up_matrix, down_matrix):
    gate_act = jnp.dot(row_block, gate_matrix, preferred_element_type=jnp.float32)
    up_act = jnp.dot(row_block, up_matrix, preferred_element_type=jnp.float32)
    hidden = (jax.nn.silu(gate_act) * up_act).astype(jnp.bfloat16)
    return jnp.dot(hidden, down_matrix, preferred_element_type=jnp.float32).astype(jnp.bfloat16)


def shards(tokens, expert_ids, gate_probs, w_gate, w_up, w_down):
    ep_count = lax.axis_size("ep")
    tok_count, features = tokens.shape
    top_count = expert_ids.shape[1]
    most = min(tok_count, 2 * tok_count * top_count // ep_count)
    gate_matrix = w_gate[0]
    up_matrix = w_up[0]
    down_matrix = w_down[0]
    flat_ids = expert_ids.reshape(-1)
    owners = jnp.arange(tok_count * top_count, dtype=jnp.int32) // top_count
    onehot = (flat_ids[:, None] == jnp.arange(ep_count, dtype=jnp.int32)[None, :]).astype(jnp.int32)
    within_rank = jnp.sum((jnp.cumsum(onehot, axis=0) - onehot) * onehot, axis=1)
    slot_index = flat_ids * most + within_rank
    slot_token = jnp.zeros((ep_count * most,), jnp.int32).at[slot_index].set(owners)
    filled = jnp.zeros((ep_count * most,), jnp.bool_).at[slot_index].set(True)
    send_rows = jnp.where(filled[:, None], tokens[slot_token], jnp.zeros((), jnp.bfloat16))
    send_rows = send_rows.reshape(ep_count, most, features)

    def serve_rows(received):
        flat_out = expert_ffn(received.reshape(-1, features), gate_matrix, up_matrix, down_matrix)
        return flat_out.reshape(received.shape)

    received = lax.all_to_all(send_rows, "ep", split_axis=0, concat_axis=0, tiled=True)
    served = serve_rows(received)
    gathered = lax.all_to_all(served, "ep", split_axis=0, concat_axis=0, tiled=True)
    picked = gathered.reshape(-1, features)[slot_index].reshape(tok_count, top_count, features)
    weights = gate_probs / jnp.sum(gate_probs, axis=1, keepdims=True)
    combined = jnp.einsum("tk,tkd->td", weights, picked.astype(jnp.float32))
    return combined.astype(jnp.bfloat16)


def solution(mesh):
    placed = (
        P(("dp", "ep"), None),
        P(("dp", "ep"), None),
        P(("dp", "ep"), None),
        P("ep", None, None),
        P("ep", None, None),
        P("ep", None, None),
    )
    return jax.shard_map(
        shards, mesh=mesh, in_specs=placed, out_specs=P(("dp", "ep"), None), check_vma=False
    )
```

profile of v0, /device:TPU:1, one launch (start us, length us, event | category | flops | bytes accessed | tf_op | source)
XLA Modules:
  0.0 178.7 jit_solution(11662310482908079254)
XLA Ops:
  0.0 0.0 copy-start
  0.0 0.0 copy-start.1
  0.0 0.9 copy.8
  0.9 0.1 eq.29
  1.0 0.1 eq.25
  1.1 0.7 broadcast_multiply_fusion
  1.8 1.2 reduce-window.6
  3.0 0.2 slice_reduce_fusion
  3.3 0.1 copy.7
  3.3 0.1 mul.28
  3.4 0.1 fusion.13
  3.6 2.4 %scatter_custom_fusion.1 = s32[1024]{0:T(1024)S(1)} fusion(s32[512]{0:T(512)S(1)} %bitcast.53, s32[512]{0:T(512)S(1)} %add_select_fusion, s32[]{:T(128)} %constant.32.clone.1), kind=kCustom, calls=%fused_computation.35 | custom fusion | bytes 4100 | tf_op jit(solution)/shard_map/scatter | solution.py:27
  6.0 2.4 %scatter_custom_fusion = pred[1024]{0:T(1024)(128)(4,1)S(1)} fusion(s32[512]{0:T(512)S(1)} %bitcast.54, pred[512]{0:T(512)(128)(4,1)S(1)} %broadcast.67, pred[]{:T(512)} %constant.30.clone.1), kind=kCustom, calls=%fused_computation.39 | custom fusion | bytes 1025 | tf_op jit(solution)/shard_map/scatter | solution.py:28
  8.5 0.1 broadcast_in_dim.31
  8.6 0.0 copy-done.1
  8.6 6.0 %gather_fusion = bf16[1024,2048]{1,0:T(8,128)(2,1)} fusion(bf16[64,2048]{1,0:T(8,128)(2,1)S(1)} %copy-done.1, s32[1024]{0:T(1024)S(1)} %fusion.15), kind=kCustom, calls=%fused_computation | custom fusion | bytes 8392704 | tf_op jit(solution)/shard_map/gather | solution.py:29
  14.6 2.5 %broadcast_select_fusion = bf16[32,32,2048]{2,1,0:T(8,128)(2,1)S(1)} fusion(bf16[32,32,2048]{2,1,0:T(8,128)(2,1)} %bitcast.49, pred[32,32]{1,0:T(8,128)(4,1)S(1)} %broadcast_in_dim.31), kind=kLoop, calls=%fused_computation.4 | loop fusion | flops 2097152 | bytes 8389632 | tf_op jit(solution)/shard_map/jit(_where)/select_n | solution.py:29
  17.1 0.0 copy-start.4
  17.1 61.3 %all_to_all.10 = bf16[32,32,2048]{2,1,0:T(8,128)(2,1)S(1)} all-to-all(bf16[32,32,2048]{2,1,0:T(8,128)(2,1)S(1)} %broadcast_select_fusion), channel_id=1, replica_groups=mesh['ep'=32,'dp'=8] {'ep'}, dimensions={0} | all-to-all | bytes 8388608 | tf_op jit(solution)/shard_map/all_to_all | solution.py:36
  78.5 2.0 %copy-done.2 = bf16[32,32,2048]{2,1,0:T(8,128)(2,1)} copy-done((bf16[32,32,2048]{2,1,0:T(8,128)(2,1)}, bf16[32,32,2048]{2,1,0:T(8,128)(2,1)S(1)}, u32[]{:S(2)}) %copy-start.2) | copy-done | bytes 4194328
  80.5 0.0 copy-done.4
  80.5 5.2 %fusion.1 = f32[1024,768]{1,0:T(8,128)} fusion(bf16[1024,2048]{1,0:T(8,128)(2,1)S(1)} %bitcast.51, bf16[1,2048,768]{2,1,0:T(8,128)(2,1)S(1)} %copy-done.4), kind=kOutput, calls=%fused_computation.7 | convolution fusion | flops 3221225472 | bytes 10485760 | tf_op jit(solution)/shard_map/dot_general | solution.py:9
  85.6 0.0 copy-done
  85.6 12.3 %convolution_convert_fusion = bf16[1024,2048]{1,0:T(8,128)(2,1)} fusion(bf16[1,768,2048]{2,1,0:T(8,128)(2,1)S(1)} %copy-done, f32[1024,768]{1,0:T(8,128)} %fusion.1, bf16[1024,2048]{1,0:T(8,128)(2,1)} %bitcast.52, bf16[1,2048,768]{2,1,0:T(8,128)(2,1)} %param.9), kind=kOutput, calls=%fused_computation.5 | convolution fusion | flops 6449266688 | bytes 17825792 | tf_op jit(solution)/shard_map/dot_general | solution.py:11
  98.0 0.0 copy-start.3
  98.0 12.3 %all-to-all-start.1 = ((bf16[32,32,2048]{2,1,0:T(8,128)(2,1)}), bf16[32,32,2048]{2,1,0:T(8,128)(2,1)}, u32[]{:S(2)}, u32[]{:S(2)}) async-start(bf16[32,32,2048]{2,1,0:T(8,128)(2,1)} %bitcast.50), calls=%async_computation.1 | async-start | bytes 8388608 | tf_op jit(solution)/shard_map/all_to_all | solution.py:38
  110.3 0.0 copy-done.3
  110.3 0.1 copy.11
  110.4 57.1 %all-to-all-done.1 = bf16[32,32,2048]{2,1,0:T(8,128)(2,1)} async-done(((bf16[32,32,2048]{2,1,0:T(8,128)(2,1)}), bf16[32,32,2048]{2,1,0:T(8,128)(2,1)}, u32[]{:S(2)}, u32[]{:S(2)}) %all-to-all-start.1) | async-done | bytes 4194336 | tf_op jit(solution)/shard_map/all_to_all | solution.py:38
  167.6 8.0 %gather_fusion.1 = bf16[512,2048]{1,0:T(8,128)(2,1)} fusion(bf16[1024,2048]{1,0:T(8,128)(2,1)} %bitcast.10, s32[1024]{0:T(1024)S(1)} %pad_clamp_fusion), kind=kCustom, calls=%fused_computation.1 | custom fusion | bytes 4196352 | tf_op jit(solution)/shard_map/gather | solution.py:39
  175.6 2.3 %fusion.7 = bf16[64,1,2048]{2,1,0:T(2,128)(2,1)S(1)} fusion(bf16[64,8,1]{1,2,0:T(2,128)(2,1)S(1)} %copy.11, bf16[512,2048]{1,0:T(8,128)(2,1)} %gather_fusion.1), kind=kOutput, calls=%fused_computation.12 | convolution fusion | flops 2097152 | bytes 2360320 | tf_op jit(solution)/shard_map/tk,tkd->td/dot_general | solution.py:41
  177.9 0.9 copy.16
  (11 shorter events, 0.1 us)
Async XLA Ops:
  0.0 85.6 %copy-start = (bf16[1,768,2048]{2,1,0:T(8,128)(2,1)S(1)}, bf16[1,768,2048]{2,1,0:T(8,128)(2,1)}, u32[]{:S(2)}) copy-start(bf16[1,768,2048]{2,1,0:T(8,128)(2,1)} %param.11) | copy-start | bytes 9437188
  0.0 8.6 %copy-start.1 = (bf16[64,2048]{1,0:T(8,128)(2,1)S(1)}, bf16[64,2048]{1,0:T(8,128)(2,1)}, u32[]{:S(2)}) copy-start(bf16[64,2048]{1,0:T(8,128)(2,1)} %param.6) | copy-start | bytes 786436
  17.1 63.3 %copy-start.4 = (bf16[1,2048,768]{2,1,0:T(8,128)(2,1)S(1)}, bf16[1,2048,768]{2,1,0:T(8,128)(2,1)}, u32[]{:S(2)}) copy-start(bf16[1,2048,768]{2,1,0:T(8,128)(2,1)} %param.10) | copy-start | bytes 9437188
  78.5 2.0 %copy-start.2 = (bf16[32,32,2048]{2,1,0:T(8,128)(2,1)}, bf16[32,32,2048]{2,1,0:T(8,128)(2,1)S(1)}, u32[]{:S(2)}) copy-start(bf16[32,32,2048]{2,1,0:T(8,128)(2,1)S(1)} %all_to_all.10) | copy-start | bytes 12582916
  98.0 12.3 %copy-start.3 = (f32[64,8]{0,1:T(8,128)S(1)}, f32[64,8]{0,1:T(8,128)}, u32[]{:S(2)}) copy-start(f32[64,8]{0,1:T(8,128)} %param.8) | copy-start | bytes 6148
  98.0 69.6 %all-to-all-start.1 = ((bf16[32,32,2048]{2,1,0:T(8,128)(2,1)}), bf16[32,32,2048]{2,1,0:T(8,128)(2,1)}, u32[]{:S(2)}, u32[]{:S(2)}) async-start(bf16[32,32,2048]{2,1,0:T(8,128)(2,1)} %bitcast.50), calls=%async_computation.1 | async-start | bytes 8388608 | tf_op jit(solution)/shard_map/all_to_all | solution.py:38
where the time goes:
time: 180 us; the launch traced here: 179 us
  blocking collectives  61.3 us (34%)
  waiting for transfers between devices  57.1 us (32%)
  local copies, waits for them, and re-layouts  23.5 us (13%)
  matrix products  19.8 us (11%)
  starting transfers between devices  12.3 us (7%)
  other arithmetic  4.6 us (3%)
    all_to_all x1, blocking collectives, shards(): lax.all_to_all(send_rows, 'ep', split_axis=0, concat_axis=0, tiled=True)  61.3 us
    all_to_all x1, waiting for transfers between devices, shards(): lax.all_to_all(served, 'ep', split_axis=0, concat_axis=0, tiled=True)  57.1 us
    dot_general x1, matrix products, expert_ffn(): jnp.dot(hidden, down_matrix, preferred_element_type=jnp.float32)  12.3 us
    all_to_all x1, starting transfers between devices, shards(): lax.all_to_all(served, 'ep', split_axis=0, concat_axis=0, tiled=True)  12.3 us
    gather x1, local copies, waits for them, and re-layouts, shards(): gathered.reshape(-1, features)[slot_index]  8.02 us
    gather x1, local copies, waits for them, and re-layouts, shards(): tokens[slot_token]  6.02 us
    dot_general x1, matrix products, expert_ffn(): up_act = jnp.dot(row_block, up_matrix, preferred_element_type=jnp.float32)  5.18 us
  transfers between devices with their start and end apart: 1, of which 1 were waited for; matrix products, arithmetic and copies ran while one was open for 0% of the time, Pallas kernels for 0%

commit v1 on v0

v1 whole, which is shorter than its diff:
```python
import functools

import jax
import jax.numpy as jnp
from jax import lax
from jax.experimental import pallas as pl
from jax.experimental.pallas import tpu as pltpu
from jax.sharding import PartitionSpec as P

MESH = pl.DeviceIdType.MESH
F32, BF16 = jnp.float32, jnp.bfloat16
OPPOSITE = {"xp": "xm", "xm": "xp", "yp": "ym", "ym": "yp", "zp": "zm", "zm": "zp"}

ORDER = [
    (0, 0), (1, 0), (3, 0), (0, 1), (0, 3), (1, 1), (1, 3), (3, 1),
    (3, 3), (0, 2), (2, 0), (1, 2), (3, 2), (2, 1), (2, 3), (2, 2),
]
PLACE = {slot: place for place, slot in enumerate(ORDER)}
CHUNKS = 4
MAX_COPIES = 176


def kernel(
    sizes, tok_hbm, ids_ref, probs_ref, wg_hbm, wu_hbm, wd_hbm, out_ref,
    gath, meta, comb, xown, zsend, zrecv, hown, hz, wg, wu, wd, zout, both, part,
    y1p, y1m, x1p, x1m, y2p, y2m, x2p, x2m, x4p, x4m, y4p, y4m, x5p, x5m, y5p, y5m,
    send_sem, recv_sem, local_sem,
):
    n_hi, tok, width, hid, most = sizes
    half, quarter = width // 2, width // 4
    ep, dp = lax.axis_index("ep"), lax.axis_index("dp")
    x, y, z_lo = lax.rem(ep, 4), lax.rem(ep // 4, 4), ep // 16
    z_hi, core = dp // 2, lax.rem(dp, 2)

    def at(xx, yy, zz):
        return zz * 16 + yy * 4 + xx

    z_up = lax.rem(z_hi + z_lo, n_hi) * 2 + core
    z_down = lax.rem(z_hi + z_lo + n_hi - 1, n_hi) * 2 + core
    target = {
        "xp": {"ep": at(lax.rem(x + 1, 4), y, z_lo), "dp": dp},
        "xm": {"ep": at(lax.rem(x + 3, 4), y, z_lo), "dp": dp},
        "yp": {"ep": at(x, lax.rem(y + 1, 4), z_lo), "dp": dp},
        "ym": {"ep": at(x, lax.rem(y + 3, 4), z_lo), "dp": dp},
        "zp": {"ep": at(x, y, 1 - z_lo), "dp": z_up},
        "zm": {"ep": at(x, y, 1 - z_lo), "dp": z_down},
    }
    other = at(x, y, 1 - z_lo)

    copies = {}

    def send(name, way, src, dst):
        index = len(copies)
        copy = pltpu.make_async_remote_copy(
            src_ref=src, dst_ref=dst, send_sem=send_sem.at[index], recv_sem=recv_sem.at[index],
            device_id=target[way], device_id_type=MESH,
        )
        copy.start()
        copies[name] = copy

    def wait(*names):
        for name in names:
            copies[name].wait_recv()

    load_tok = pltpu.make_async_copy(tok_hbm, gath.at[0, 0], local_sem.at[0])
    load_tok.start()
    loads = [
        pltpu.make_async_copy(src.at[0], dst, local_sem.at[1 + i])
        for i, (src, dst) in enumerate(((wg_hbm, wg), (wu_hbm, wu), (wd_hbm, wd)))
    ]
    for load in loads:
        load.start()

    barrier = pltpu.get_barrier_semaphore()
    for way in target:
        pl.semaphore_signal(barrier, inc=1, device_id=target[way], device_id_type=MESH)

    ids = ids_ref[...].astype(F32)
    probs = probs_ref[...]
    weights = probs / jnp.sum(probs, axis=0, keepdims=True)
    experts = lax.broadcasted_iota(jnp.int32, (32, tok), 0).astype(F32)
    named = jnp.zeros((32, tok), F32)
    for k in range(8):
        named = named + jnp.where(ids[k:k + 1, :] == experts, 1.0, 0.0)
    before = lax.broadcasted_iota(jnp.int32, (tok, tok), 0) < lax.broadcasted_iota(jnp.int32, (tok, tok), 1)
    ranks = jnp.dot(named.astype(BF16), before.astype(F32).astype(BF16), preferred_element_type=F32)
    for k in range(8):
        rank = jnp.sum(jnp.where(ids[k:k + 1, :] == experts, ranks, 0.0), axis=0, keepdims=True)
        meta[0, 0, k:k + 1, 0:tok] = ids[k:k + 1, :] * float(most) + rank
    meta[0, 0, 8:16, 0:tok] = weights

    pl.semaphore_wait(barrier, 6)
    load_tok.wait()

    first, second = pl.ds(0, half), pl.ds(half, half)
    quarters = [pl.ds(q * quarter, quarter) for q in range(4)]

    def move(tag, way, slot, cols, with_meta=False):
        dx, dy = slot
        shift = {"xp": (3, 0), "xm": (1, 0), "yp": (0, 3), "ym": (0, 1)}[way]
        to = ((dx + shift[0]) % 4, (dy + shift[1]) % 4)
        send((tag, way, to), way, gath.at[dx, dy, :, cols], gath.at[to[0], to[1], :, cols])
        if with_meta:
            send(("m" + tag, way, to), way, meta.at[dx, dy], meta.at[to[0], to[1]])

    def x_own():
        move("a", "xp", (0, 0), first, True)
        move("a", "xm", (0, 0), first, True)

    def y_own():
        move("b", "yp", (0, 0), second)
        move("b", "ym", (0, 0), second)

    def y_pass(dx):
        move("c", "yp", (dx, 0), first, True)
        move("c", "ym", (dx, 0), first, True)

    def x_pass(dy):
        move("d", "xp", (0, dy), second)
        move("d", "xm", (0, dy), second)

    def x_relay():
        move("e", "xp", (3, 0), quarters[0], True)
        move("e", "xm", (1, 0), quarters[1])

    def y_relay():
        move("f", "yp", (0, 3), quarters[2])
        move("f", "ym", (0, 1), quarters[3])

    def y_pass_relay(dx):
        move("g", "yp", (dx, 3), quarters[0], True)
        move("g", "ym", (dx, 1), quarters[1])

    def x_pass_relay(dy):
        move("h", "xp", (3, dy), quarters[2])
        move("h", "xm", (1, dy), quarters[3])

    def got_y_pass(dx):
        wait(("c", "yp", (dx, 3)), ("mc", "yp", (dx, 3)), ("c", "ym", (dx, 1)), ("mc", "ym", (dx, 1)))

    def got_x_pass(dy):
        wait(("d", "xp", (3, dy)), ("d", "xm", (1, dy)))

    def got_y_pass_relay(dx):
        wait(("g", "yp", (dx, 2)), ("mg", "yp", (dx, 2)), ("g", "ym", (dx, 2)))

    def got_x_pass_relay(dy):
        wait(("h", "xp", (2, dy)), ("h", "xm", (2, dy)))

    place_row = lax.broadcasted_iota(jnp.int32, (2 * most, tok), 0)
    wanted = jnp.where(place_row < most, ep * most + place_row, (other - 1) * most + place_row).astype(F32)

    def select(dx, dy):
        place = PLACE[dx, dy]
        one, scaled = jnp.zeros((2 * most, tok), F32), jnp.zeros((2 * most, tok), F32)
        for k in range(8):
            hit = meta[dx, dy, k:k + 1, 0:tok] == wanted
            one = one + jnp.where(hit, 1.0, 0.0)
            scaled = scaled + jnp.where(hit, meta[dx, dy, 8 + k:9 + k, 0:tok], 0.0)
        comb[place] = scaled.T.astype(BF16)
        pick = one.astype(BF16)

        @pl.loop(0, 4)
        def _(q):
            cols = pl.ds(pl.multiple_of(q * quarter, quarter), quarter)
            rows = jnp.dot(pick, gath[dx, dy, :, cols], preferred_element_type=F32).astype(BF16)
            xown[place, :, cols] = rows[:most]
            zsend[place, :, cols] = rows[most:]

        send(("z", place), "zm" if place % 2 else "zp", zsend.at[place], zrecv.at[place])

    def gate_up(rows_ref, group, hidden):
        rows = 8 * most
        tile = 256

        @pl.loop(0, hid // tile)
        def _(n):
            cols = pl.ds(pl.multiple_of(n * tile, tile), tile)
            block = rows_ref[8 * group:8 * group + 8].reshape(rows, width)
            gate = jnp.dot(block, wg[:, cols], preferred_element_type=F32)
            up = jnp.dot(block, wu[:, cols], preferred_element_type=F32)
            hidden[rows * group:rows * (group + 1), cols] = (gate / (1.0 + jnp.exp(-gate)) * up).astype(BF16)

    x_own()
    y_own()
    y_pass(0)
    x_pass(0)
    select(0, 0)
    wait(("a", "xp", (3, 0)), ("ma", "xp", (3, 0)), ("a", "xm", (1, 0)), ("ma", "xm", (1, 0)))
    wait(("b", "yp", (0, 3)), ("b", "ym", (0, 1)))
    x_relay()
    y_relay()
    for d in (1, 3):
        y_pass(d)
        x_pass(d)
    got_y_pass(0)
    got_x_pass(0)
    y_pass_relay(0)
    x_pass_relay(0)
    for slot in ORDER[1:5]:
        select(*slot)
    wait(("e", "xp", (2, 0)), ("me", "xp", (2, 0)), ("e", "xm", (2, 0)))
    wait(("f", "yp", (0, 2)), ("f", "ym", (0, 2)))
    y_pass(2)
    x_pass(2)
    for d in (1, 3):
        got_y_pass(d)
        got_x_pass(d)
        y_pass_relay(d)
        x_pass_relay(d)
    for slot in ORDER[5:9]:
        select(*slot)
    got_y_pass_relay(0)
    got_x_pass_relay(0)
    for slot in ORDER[9:11]:
        select(*slot)
    got_y_pass(2)
    got_x_pass(2)
    y_pass_relay(2)
    x_pass_relay(2)
    loads[0].wait()
    loads[1].wait()
    gate_up(xown, 0, hown)
    for d in (1, 3):
        got_y_pass_relay(d)
        got_x_pass_relay(d)
    for slot in ORDER[11:15]:
        select(*slot)
    got_y_pass_relay(2)
    got_x_pass_relay(2)
    select(2, 2)

    def chunk_cols(c):
        return pl.ds(c * (width // CHUNKS), width // CHUNKS)

    def down_z(group, c):
        rows = 8 * most
        out = jnp.dot(hz[rows * group:rows * (group + 1), :], wd[:, chunk_cols(c)], preferred_element_type=F32)
        zout[4 * group:4 * group + 4, :, :, chunk_cols(c)] = out.astype(BF16).reshape(4, 2, most, width // CHUNKS)
        for side, way in ((0, "zm"), (1, "zp")):
            send(
                ("r", group, c, side), way,
                zout.at[pl.ds(4 * group, 4), side, :, chunk_cols(c)],
                both.at[pl.ds(4 * group, 4), side, pl.ds(most, most), chunk_cols(c)],
            )

    def down_own(c):
        out = jnp.dot(hown[...], wd[:, chunk_cols(c)], preferred_element_type=F32)
        both[:, :, 0:most, chunk_cols(c)] = out.astype(BF16).reshape(8, 2, most, width // CHUNKS)

    for place in range(8):
        wait(("z", place))
    gate_up(zrecv, 0, hz)
    loads[2].wait()
    down_z(0, 0)
    down_z(0, 1)
    gate_up(xown, 1, hown)
    for place in range(8, 16):
        wait(("z", place))
    gate_up(zrecv, 1, hz)
    down_z(1, 0)
    down_z(1, 1)
    for c in (2, 3):
        down_z(0, c)
        down_z(1, c)
    for c in range(CHUNKS):
        down_own(c)

    unit = width // CHUNKS // 4

    def cols_of(c, start, count=1):
        return pl.ds((4 * c + start) * unit, count * unit)

    def expand(c):
        cols = chunk_cols(c)
        for group in (0, 1):
            wait(("r", group, c, 0), ("r", group, c, 1))

        def fill(dx, dy):
            place = PLACE[dx, dy]
            part[dx, dy, :, cols] = jnp.dot(
                comb[place], both[place // 2, place % 2, :, cols], preferred_element_type=F32
            ).astype(BF16)

        far = [slot for slot in ORDER if 2 in slot]
        for slot in far:
            fill(*slot)
        send(("1", c, "yp"), "yp", part.at[:, 2, :, cols_of(c, 0)], y1p.at[c])
        send(("1", c, "ym"), "ym", part.at[:, 2, :, cols_of(c, 1)], y1m.at[c])
        send(("1", c, "xp"), "xp", part.at[2, :, :, cols_of(c, 2)], x1p.at[c])
        send(("1", c, "xm"), "xm", part.at[2, :, :, cols_of(c, 3)], x1m.at[c])
        for slot in ORDER:
            if slot not in far:
                fill(*slot)

    def add(dx, dy, cols, *refs):
        total = part[dx, dy, :, cols].astype(F32)
        for ref in refs:
            total = total + ref[...].astype(F32)
        part[dx, dy, :, cols] = total.astype(BF16)

    def step_two(c):
        for way in ("yp", "ym", "xp", "xm"):
            wait(("1", c, way))
        for d in range(4):
            add(d, 1, cols_of(c, 0), y1p.at[c, d])
            add(d, 3, cols_of(c, 1), y1m.at[c, d])
            add(1, d, cols_of(c, 2), x1p.at[c, d])
            add(3, d, cols_of(c, 3), x1m.at[c, d])
        send(("2", c, "yp"), "yp", part.at[:, 1, :, cols_of(c, 0, 2)], y2p.at[c])
        send(("2", c, "ym"), "ym", part.at[:, 3, :, cols_of(c, 0, 2)], y2m.at[c])
        send(("2", c, "xp"), "xp", part.at[1, :, :, cols_of(c, 2, 2)], x2p.at[c])
        send(("2", c, "xm"), "xm", part.at[3, :, :, cols_of(c, 2, 2)], x2m.at[c])

    def step_three(c):
        for way in ("yp", "ym", "xp", "xm"):
            wait(("2", c, way))
        for d in (2, 1, 3, 0):
            add(d, 0, cols_of(c, 0, 2), y2p.at[c, d], y2m.at[c, d])
            add(0, d, cols_of(c, 2, 2), x2p.at[c, d], x2m.at[c, d])
            if d == 2:
                send(("4", c, "xp"), "xp", part.at[2, 0, :, cols_of(c, 0)], x4p.at[c])
                send(("4", c, "xm"), "xm", part.at[2, 0, :, cols_of(c, 1)], x4m.at[c])
                send(("4", c, "yp"), "yp", part.at[0, 2, :, cols_of(c, 2)], y4p.at[c])
                send(("4", c, "ym"), "ym", part.at[0, 2, :, cols_of(c, 3)], y4m.at[c])

    def step_four(c):
        for way in ("xp", "xm", "yp", "ym"):
            wait(("4", c, way))
        add(1, 0, cols_of(c, 0), x4p.at[c])
        add(3, 0, cols_of(c, 1), x4m.at[c])
        add(0, 1, cols_of(c, 2), y4p.at[c])
        add(0, 3, cols_of(c, 3), y4m.at[c])
        send(("5", c, "xp"), "xp", part.at[1, 0, :, cols_of(c, 0, 2)], x5p.at[c])
        send(("5", c, "xm"), "xm", part.at[3, 0, :, cols_of(c, 0, 2)], x5m.at[c])
        send(("5", c, "yp"), "yp", part.at[0, 1, :, cols_of(c, 2, 2)], y5p.at[c])
        send(("5", c, "ym"), "ym", part.at[0, 3, :, cols_of(c, 2, 2)], y5m.at[c])

    def step_five(c):
        for way in ("xp", "xm", "yp", "ym"):
            wait(("5", c, way))
        for start, plus, minus in ((0, x5p, x5m), (2, y5p, y5m)):
            cols = cols_of(c, start, 2)
            total = part[0, 0, :, cols].astype(F32) + plus[c].astype(F32) + minus[c].astype(F32)
            out_ref[:, cols] = total.astype(BF16)

    expand(0)
    step_two(0)
    expand(1)
    step_three(0)
    step_two(1)
    step_four(0)
    expand(2)
    step_three(1)
    step_two(2)
    step_five(0)
    step_four(1)
    expand(3)
    step_three(2)
    step_two(3)
    step_five(1)
    step_four(2)
    step_three(3)
    step_five(2)
    step_four(3)
    step_five(3)
    for copy in copies.values():
        copy.wait_send()


def shards(n_hi, tokens, expert_ids, gate_probs, w_gate, w_up, w_down):
    tok, width = tokens.shape
    hid = w_gate.shape[2]
    most = 32
    unit = width // CHUNKS // 4
    vmem = pl.BlockSpec(memory_space=pltpu.VMEM)
    hbm = pl.BlockSpec(memory_space=pl.ANY)
    wide = [pltpu.VMEM((CHUNKS, 4, tok, unit), BF16)] * 4 + [pltpu.VMEM((CHUNKS, 4, tok, 2 * unit), BF16)] * 4
    thin = [pltpu.VMEM((CHUNKS, tok, unit), BF16)] * 4 + [pltpu.VMEM((CHUNKS, tok, 2 * unit), BF16)] * 4
    return pl.pallas_call(
        functools.partial(kernel, (n_hi, tok, width, hid, most)),
        out_shape=jax.ShapeDtypeStruct((tok, width), BF16),
        in_specs=[hbm, vmem, vmem, hbm, hbm, hbm],
        out_specs=vmem,
        scratch_shapes=[
            pltpu.VMEM((4, 4, tok, width), BF16),
            pltpu.VMEM((4, 4, 16, 128), F32),
            pltpu.VMEM((16, tok, 2 * most), BF16),
            pltpu.VMEM((16, most, width), BF16),
            pltpu.VMEM((16, most, width), BF16),
            pltpu.VMEM((16, most, width), BF16),
            pltpu.VMEM((16 * most, hid), BF16),
            pltpu.VMEM((16 * most, hid), BF16),
            pltpu.VMEM((width, hid), BF16),
            pltpu.VMEM((width, hid), BF16),
            pltpu.VMEM((hid, width), BF16),
            pltpu.VMEM((8, 2, most, width), BF16),
            pltpu.VMEM((8, 2, 2 * most, width), BF16),
            pltpu.VMEM((4, 4, tok, width), BF16),
            *wide,
            *thin,
            pltpu.SemaphoreType.DMA((MAX_COPIES,)),
            pltpu.SemaphoreType.DMA((MAX_COPIES,)),
            pltpu.SemaphoreType.DMA((4,)),
        ],
        compiler_params=pltpu.CompilerParams(
            collective_id=0, has_side_effects=True, vmem_limit_bytes=60 * 1024 * 1024
        ),
        name="routed_experts",
    )(tokens, expert_ids.T, gate_probs.T, w_gate, w_up, w_down)


def solution(mesh):
    placed = (
        P(("dp", "ep"), None),
        P(("dp", "ep"), None),
        P(("dp", "ep"), None),
        P("ep", None, None),
        P("ep", None, None),
        P("ep", None, None),
    )
    return jax.shard_map(
        functools.partial(shards, mesh.shape["dp"] // 2), mesh=mesh, in_specs=placed,
        out_specs=P(("dp", "ep"), None), check_vma=False,
    )
```

time: 180 us -> 95 us (0.53)
  the two profiles are of different devices: /device:TPU:1 before, /device:TPU:64 now
where the time goes in v1:
time: 95 us; the launch traced here: 94.8 us
  Pallas kernels  93.2 us (98%)
  local copies, waits for them, and re-layouts  1.67 us (2%)
    pallas_call x1, Pallas kernels, shards(): pl.pallas_call(functools.partial(kernel, (n_hi, tok, width, hid, most)),...  93.2 us

profile of v1, /device:TPU:64, one launch (start us, length us, event | category | flops | bytes accessed | tf_op | source)
XLA Modules:
  0.0 94.8 jit_solution(7455501880452946191)
XLA Ops:
  0.0 93.2 %routed_experts.1 = bf16[64,2048]{1,0:T(8,128)(2,1)} custom-call(bf16[64,2048]{1,0:T(8,128)(2,1)} %tok_hbm.1, s32[8,64]{1,0:T(8,128)} %bitcast.2, f32[8,64]{1,0:T(8,128)} %bitcast.3, bf16[1,2048,768]{2,1,0:T(8,128)(2,1)} %wg_hbm.1, bf16[1,2048,768]{2,1,0:T(8,128)(2,1)} %wu_hbm.1, bf16[1,768,2048]{2,1,0:T(8,128)(2,1)} %wd_hbm.1), custom_call_target="tpu_custom_call" | custom-call | tf_op jit(solution)/shard_map/routed_experts/pallas_call | solution.py:380
  93.2 1.7 %copy.8 = bf16[64,2048]{1,0:T(8,128)(2,1)} copy(bf16[64,2048]{1,0:T(8,128)(2,1)} %routed_experts.1) | data formatting | bytes 524288

commit v2 on v0

v2 whole, which is shorter than its diff:
```python
import functools

import jax
import jax.numpy as jnp
from jax import lax
from jax.experimental import pallas as pl
from jax.experimental.pallas import tpu as pltpu
from jax.sharding import PartitionSpec as P

MESH = pl.DeviceIdType.MESH
F32, BF16 = jnp.float32, jnp.bfloat16
OPPOSITE = {"xp": "xm", "xm": "xp", "yp": "ym", "ym": "yp", "zp": "zm", "zm": "zp"}

ORDER = [
    (0, 0), (1, 0), (3, 0), (0, 1), (0, 3), (1, 1), (1, 3), (3, 1),
    (3, 3), (0, 2), (2, 0), (1, 2), (3, 2), (2, 1), (2, 3), (2, 2),
]
PLACE = {slot: place for place, slot in enumerate(ORDER)}
PARTS = (2, 2, 2, 1, 1)
STEPS = (
    "E0", "E1", "A0", "A1", "E2", "B0", "B1", "E3", "A2", "E4", "C0", "C1", "A3", "B2", "A4", "D0", "D1", "B3", "C2", "B4",
    "C3", "D2", "C4", "D3", "D4",
)
MAX_SEMS = 64


def kernel(
    sizes, tok_hbm, ids_ref, probs_ref, wg_hbm, wu_hbm, wd_hbm, out_hbm,
    gath, meta, comb, xown, zsend, zrecv, hown, hz, wg, wu, wd, zout, both, part, picks,
    r1p, r1m, r2p, r2m, r4p, r4m, r5p, r5m, outv,
    send_sem, recv_sem, local_sem,
):
    n_hi, tok, width, hid, most = sizes
    half, quarter = width // 2, width // 4
    ep, dp = lax.axis_index("ep"), lax.axis_index("dp")
    x, y, z_lo = lax.rem(ep, 4), lax.rem(ep // 4, 4), ep // 16
    z_hi, core = dp // 2, lax.rem(dp, 2)

    def at(xx, yy, zz):
        return zz * 16 + yy * 4 + xx

    cross = 1 - core
    here = z_hi * 2 + cross
    z_up = lax.rem(z_hi + z_lo, n_hi) * 2 + cross
    z_down = lax.rem(z_hi + z_lo + n_hi - 1, n_hi) * 2 + cross
    target = {
        "xp": {"ep": at(lax.rem(x + 1, 4), y, z_lo), "dp": here},
        "xm": {"ep": at(lax.rem(x + 3, 4), y, z_lo), "dp": here},
        "yp": {"ep": at(x, lax.rem(y + 1, 4), z_lo), "dp": here},
        "ym": {"ep": at(x, lax.rem(y + 3, 4), z_lo), "dp": here},
        "zp": {"ep": at(x, y, 1 - z_lo), "dp": z_up},
        "zm": {"ep": at(x, y, 1 - z_lo), "dp": z_down},
    }
    other = at(x, y, 1 - z_lo)

    sems = {}

    def sem(array, kind):
        return array.at[sems.setdefault(kind, len(sems))]

    def send(way, src, dst, leaves, lands):
        pltpu.make_async_remote_copy(
            src_ref=src, dst_ref=dst, send_sem=sem(send_sem, leaves), recv_sem=sem(recv_sem, lands),
            device_id=target[way], device_id_type=MESH,
        ).start()

    def wait(lands, *like):
        pltpu.make_async_copy(*like, *like, sem(recv_sem, lands)).wait()

    def drain(leaves, like):
        pltpu.make_async_copy(like, like, sem(send_sem, leaves)).wait()

    load_tok = pltpu.make_async_copy(tok_hbm, gath.at[0, 0], local_sem.at[0])
    load_tok.start()
    loads = [
        pltpu.make_async_copy(src.at[0], dst, local_sem.at[1 + i])
        for i, (src, dst) in enumerate(((wg_hbm, wg), (wu_hbm, wu), (wd_hbm, wd)))
    ]
    for load in loads:
        load.start()

    barrier = pltpu.get_barrier_semaphore()
    for way in target:
        pl.semaphore_signal(barrier, inc=1, device_id=target[way], device_id_type=MESH)

    ids = ids_ref[...].astype(F32)
    probs = probs_ref[...]
    weights = probs / jnp.sum(probs, axis=0, keepdims=True)
    experts = lax.broadcasted_iota(jnp.int32, (32, tok), 0).astype(F32)
    named = jnp.zeros((32, tok), F32)
    for k in range(8):
        named = named + jnp.where(ids[k:k + 1, :] == experts, 1.0, 0.0)
    before = lax.broadcasted_iota(jnp.int32, (tok, tok), 0) < lax.broadcasted_iota(jnp.int32, (tok, tok), 1)
    ranks = jnp.dot(named.astype(BF16), before.astype(F32).astype(BF16), preferred_element_type=F32)
    for k in range(8):
        rank = jnp.sum(jnp.where(ids[k:k + 1, :] == experts, ranks, 0.0), axis=0, keepdims=True)
        meta[0, 0, k:k + 1, 0:tok] = ids[k:k + 1, :] * float(most) + rank
    meta[0, 0, 8:16, 0:tok] = weights

    pl.semaphore_wait(barrier, 6)
    load_tok.wait()

    first, second = pl.ds(0, half), pl.ds(half, half)
    quarters = [pl.ds(q * quarter, quarter) for q in range(4)]

    def move(kind, leaves, way, slot, cols, with_meta=None):
        dx, dy = slot
        shift = {"xp": (3, 0), "xm": (1, 0), "yp": (0, 3), "ym": (0, 1)}[way]
        to = ((dx + shift[0]) % 4, (dy + shift[1]) % 4)
        send(way, gath.at[dx, dy, :, cols], gath.at[to[0], to[1], :, cols], leaves, kind)
        if with_meta:
            send(way, meta.at[dx, dy], meta.at[to[0], to[1]], with_meta, "m" + kind)

    def own_first():
        for way in ("xp", "xm"):
            move("own", "own", way, (0, 0), first, "m12")
        for way in ("yp", "ym"):
            move("own", "own", way, (0, 0), second, "m3")

    def own_second():
        for way in ("yp", "ym"):
            move("pass0", "own", way, (0, 0), first)
        for way in ("xp", "xm"):
            move("pass0", "own", way, (0, 0), second)

    def own_relay():
        move("far", "pass", "xp", (3, 0), quarters[0], "m12")
        move("far", "pass", "xm", (1, 0), quarters[1])
        move("far", "pass", "yp", (0, 3), quarters[2], "m3")
        move("far", "pass", "ym", (0, 1), quarters[3])

    def passes(d):
        move(f"pass{d}", "pass", "yp", (d, 0), first, "m12")
        move(f"pass{d}", "pass", "ym", (d, 0), first, "m12")
        move(f"pass{d}", "second", "xp", (0, d), second)
        move(f"pass{d}", "second", "xm", (0, d), second)

    def relays(d):
        move(f"relay{d}", "relay", "yp", (d, 3), quarters[0], "m12" if d else None)
        move(f"relay{d}", "relay", "ym", (d, 1), quarters[1])
        move(f"relay{d}", "relay", "xp", (3, d), quarters[2])
        move(f"relay{d}", "relay", "xm", (1, d), quarters[3])

    def got_own():
        wait("own", gath.at[0, 0:2])
        wait("mown", meta.at[0])

    def got_far():
        wait("far", gath.at[0, 0])
        wait("mfar", meta.at[0, 0:2])

    def got_passes(d):
        wait(f"pass{d}", gath.at[0, 0:2])
        if d:
            wait(f"mpass{d}", meta.at[0, 0:2])

    def got_relays(d):
        wait(f"relay{d}", gath.at[0, 0])
        if d:
            wait(f"mrelay{d}", meta.at[0, 0])

    place_row = lax.broadcasted_iota(jnp.int32, (2 * most, tok), 0)
    wanted = jnp.where(place_row < most, ep * most + place_row, (other - 1) * most + place_row).astype(F32)

    def build(dx, dy):
        place = PLACE[dx, dy]
        one, scaled = jnp.zeros((2 * most, tok), F32), jnp.zeros((2 * most, tok), F32)
        for k in range(8):
            hit = meta[dx, dy, k:k + 1, 0:tok] == wanted
            one = one + jnp.where(hit, 1.0, 0.0)
            scaled = scaled + jnp.where(hit, meta[dx, dy, 8 + k:9 + k, 0:tok], 0.0)
        comb[place] = scaled.T.astype(BF16)
        picks[place] = one.astype(BF16)

    def select(dx, dy, side):
        place = PLACE[dx, dy]

        @pl.loop(0, 2)
        def _(q):
            cols = pl.ds(pl.multiple_of(side * half + q * quarter, quarter), quarter)
            rows = jnp.dot(picks[place], gath[dx, dy, :, cols], preferred_element_type=F32).astype(BF16)
            xown[place, :, cols] = rows[:most]
            zsend[place, :, cols] = rows[most:]

        cols = (first, second)[side]
        way = "zm" if place % 2 else "zp"
        send(way, zsend.at[place, :, cols], zrecv.at[place, :, cols], "rows", f"rows{place // 4}")

    def select_all(*slots):
        for slot in slots:
            build(*slot)
            select(*slot, 0)
            select(*slot, 1)

    def got_rows(group):
        wait(f"rows{group}", zrecv.at[pl.ds(4 * group, 4)])

    tile = 256

    def gate_up(rows_ref, hidden, place, places, start=0, stop=hid // tile):
        rows = places * most

        @pl.loop(start, stop)
        def _(n):
            cols = pl.ds(pl.multiple_of(n * tile, tile), tile)
            block = rows_ref[place:place + places].reshape(rows, width)
            gate = jnp.dot(block, wg[:, cols], preferred_element_type=F32)
            up = jnp.dot(block, wu[:, cols], preferred_element_type=F32)
            hidden[place * most:place * most + rows, cols] = (gate / (1.0 + jnp.exp(-gate)) * up).astype(BF16)

    own_first()
    own_second()
    select_all((0, 0))
    got_own()
    own_relay()
    passes(1)
    passes(3)
    for slot in ORDER[1:5]:
        build(*slot)
        select(*slot, 0 if slot[1] == 0 else 1)
    got_passes(0)
    relays(0)
    for slot in ORDER[1:5]:
        select(*slot, 1 if slot[1] == 0 else 0)
    got_far()
    passes(2)
    got_passes(1)
    relays(1)
    select_all((1, 1))
    got_passes(3)
    relays(3)
    select_all((1, 3), (3, 1), (3, 3))
    got_relays(0)
    select_all((0, 2), (2, 0))
    loads[0].wait()
    loads[1].wait()
    gate_up(xown, hown, 0, 8, 0, 1)
    got_passes(2)
    relays(2)
    gate_up(xown, hown, 0, 8, 1, 2)
    got_relays(1)
    select_all((1, 2), (2, 1))
    got_relays(3)
    select_all((3, 2), (2, 3))
    gate_up(xown, hown, 0, 8, 2, 3)
    got_relays(2)
    select_all((2, 2))

    starts = [sum(PARTS[:c]) * width // sum(PARTS) for c in range(len(PARTS) + 1)]

    def chunk_cols(c):
        return pl.ds(starts[c], starts[c + 1] - starts[c])

    def sides(c):
        middle = (starts[c] + starts[c + 1]) // 2
        return pl.ds(starts[c], middle - starts[c]), pl.ds(middle, starts[c + 1] - middle)

    top, low = pl.ds(0, tok // 2), pl.ds(tok // 2, tok // 2)

    def down_z(group, c):
        rows = 8 * most
        out = jnp.dot(hz[rows * group:rows * (group + 1), :], wd[:, chunk_cols(c)], preferred_element_type=F32)
        zout[4 * group:4 * group + 4, :, :, chunk_cols(c)] = out.astype(BF16).reshape(4, 2, most, chunk_cols(c).size)
        for side, way in ((0, "zm"), (1, "zp")):
            send(
                way,
                zout.at[pl.ds(4 * group, 4), side, :, chunk_cols(c)],
                both.at[pl.ds(4 * group, 4), side, pl.ds(most, most), chunk_cols(c)],
                "back", f"back{c}",
            )

    def down_own(c):
        out = jnp.dot(hown[...], wd[:, chunk_cols(c)], preferred_element_type=F32)
        both[:, :, 0:most, chunk_cols(c)] = out.astype(BF16).reshape(8, 2, most, chunk_cols(c).size)

    got_rows(0)
    got_rows(1)
    gate_up(zrecv, hz, 0, 8)
    loads[2].wait()
    down_z(0, 0)
    down_z(0, 1)
    gate_up(xown, hown, 8, 8)
    got_rows(2)
    gate_up(zrecv, hz, 8, 4)
    down_own(0)
    down_own(1)
    got_rows(3)
    gate_up(zrecv, hz, 12, 4)
    down_z(1, 0)
    down_z(1, 1)
    for c in range(2, len(PARTS)):
        down_z(0, c)
        down_z(1, c)

    def expand(c):
        cols = chunk_cols(c)
        left, right = sides(c)
        if c >= 2:
            down_own(c)
        wait(f"back{c}", zout.at[:, :, :, cols])

        def fill(dx, dy):
            place = PLACE[dx, dy]
            part[dx, dy, :, cols] = jnp.dot(
                comb[place], both[place // 2, place % 2, :, cols], preferred_element_type=F32
            ).astype(BF16)

        far = [slot for slot in ORDER if 2 in slot]
        for slot in far:
            fill(*slot)
        send("yp", part.at[:, 2, top, left], r1p.at[:, :, left], "1p", f"1{c}")
        send("ym", part.at[:, 2, low, left], r1m.at[:, :, left], "1m", f"1{c}")
        send("xp", part.at[2, :, top, right], r1p.at[:, :, right], "1p", f"1{c}")
        send("xm", part.at[2, :, low, right], r1m.at[:, :, right], "1m", f"1{c}")
        for slot in ORDER:
            if slot not in far:
                fill(*slot)
        halves_two(c, low, top)

    def halves_two(c, plus, minus):
        left, right = sides(c)
        send("yp", part.at[:, 1, plus, left], r2p.at[:, plus, left], "2p", f"2{c}")
        send("ym", part.at[:, 3, minus, left], r2m.at[:, minus, left], "2m", f"2{c}")
        send("xp", part.at[1, :, plus, right], r2p.at[:, plus, right], "2p", f"2{c}")
        send("xm", part.at[3, :, minus, right], r2m.at[:, minus, right], "2m", f"2{c}")

    def halves_five(c, plus, minus):
        left, right = sides(c)
        send("xp", part.at[1, 0, plus, left], r5p.at[plus, left], "5p", f"5{c}")
        send("xm", part.at[3, 0, minus, left], r5m.at[minus, left], "5m", f"5{c}")
        send("yp", part.at[0, 1, plus, right], r5p.at[plus, right], "5p", f"5{c}")
        send("ym", part.at[0, 3, minus, right], r5m.at[minus, right], "5m", f"5{c}")

    def double(c):
        return pl.ds(0, 2 * chunk_cols(c).size)

    def add(dx, dy, rows, cols, *refs):
        total = part[dx, dy, rows, cols].astype(F32)
        for ref in refs:
            total = total + ref[...].astype(F32)
        part[dx, dy, rows, cols] = total.astype(BF16)

    every = pl.ds(0, tok)

    def step_two(c):
        left, right = sides(c)
        wait(f"1{c}", r1p.at[:, :, double(c)])
        for d in range(4):
            add(d, 1, top, left, r1p.at[d, :, left])
            add(d, 3, low, left, r1m.at[d, :, left])
            add(1, d, top, right, r1p.at[d, :, right])
            add(3, d, low, right, r1m.at[d, :, right])
        halves_two(c, top, low)

    def step_three(c):
        left, right = sides(c)
        wait(f"2{c}", r2p.at[:, :, double(c)])
        for d in (2, 1, 3, 0):
            add(d, 0, every, left, r2p.at[d, :, left], r2m.at[d, :, left])
            add(0, d, every, right, r2p.at[d, :, right], r2m.at[d, :, right])
            if d == 2:
                send("xp", part.at[2, 0, top, left], r4p.at[:, left], "4p", f"4{c}")
                send("xm", part.at[2, 0, low, left], r4m.at[:, left], "4m", f"4{c}")
                send("yp", part.at[0, 2, top, right], r4p.at[:, right], "4p", f"4{c}")
                send("ym", part.at[0, 2, low, right], r4m.at[:, right], "4m", f"4{c}")
            if d == 3:
                halves_five(c, low, top)

    def step_four(c):
        left, right = sides(c)
        wait(f"4{c}", r4p.at[:, double(c)])
        add(1, 0, top, left, r4p.at[:, left])
        add(3, 0, low, left, r4m.at[:, left])
        add(0, 1, top, right, r4p.at[:, right])
        add(0, 3, low, right, r4m.at[:, right])
        halves_five(c, top, low)

    stores = []

    def step_five(c):
        wait(f"5{c}", r5p.at[:, double(c)])
        for cols in sides(c):
            total = part[0, 0, :, cols].astype(F32) + r5p[:, cols].astype(F32) + r5m[:, cols].astype(F32)
            outv[:, cols] = total.astype(BF16)
        cols = chunk_cols(c)
        store = pltpu.make_async_copy(outv.at[:, cols], out_hbm.at[:, cols], local_sem.at[4 + c])
        store.start()
        stores.append(store)

    run = {"E": expand, "A": step_two, "B": step_three, "C": step_four, "D": step_five}
    for step in STEPS:
        run[step[0]](int(step[1]))
    drain("own", gath.at[0])
    drain("pass", gath.at[0])
    drain("second", gath.at[0, 0:3])
    drain("relay", gath.at[0])
    drain("m12", meta.at[0:3])
    drain("m3", meta.at[0, 0:3])
    drain("rows", zsend)
    drain("back", zout)
    for kind, like in (("1p", r1p), ("1m", r1m), ("2p", r2p), ("2m", r2m), ("4p", r4p), ("4m", r4m), ("5p", r5p), ("5m", r5m)):
        drain(kind, like)
    for store in stores:
        store.wait()


def shards(n_hi, tokens, expert_ids, gate_probs, w_gate, w_up, w_down):
    tok, width = tokens.shape
    hid = w_gate.shape[2]
    most = 32
    vmem = pl.BlockSpec(memory_space=pltpu.VMEM)
    hbm = pl.BlockSpec(memory_space=pl.ANY)
    return pl.pallas_call(
        functools.partial(kernel, (n_hi, tok, width, hid, most)),
        out_shape=jax.ShapeDtypeStruct((tok, width), BF16),
        in_specs=[hbm, vmem, vmem, hbm, hbm, hbm],
        out_specs=hbm,
        scratch_shapes=[
            pltpu.VMEM((4, 4, tok, width), BF16),
            pltpu.VMEM((4, 4, 16, 128), F32),
            pltpu.VMEM((16, tok, 2 * most), BF16),
            pltpu.VMEM((16, most, width), BF16),
            pltpu.VMEM((16, most, width), BF16),
            pltpu.VMEM((16, most, width), BF16),
            pltpu.VMEM((16 * most, hid), BF16),
            pltpu.VMEM((16 * most, hid), BF16),
            pltpu.VMEM((width, hid), BF16),
            pltpu.VMEM((width, hid), BF16),
            pltpu.VMEM((hid, width), BF16),
            pltpu.VMEM((8, 2, most, width), BF16),
            pltpu.VMEM((8, 2, 2 * most, width), BF16),
            pltpu.VMEM((4, 4, tok, width), BF16),
            pltpu.VMEM((16, 2 * most, tok), BF16),
            pltpu.VMEM((4, tok // 2, width), BF16),
            pltpu.VMEM((4, tok // 2, width), BF16),
            pltpu.VMEM((4, tok, width), BF16),
            pltpu.VMEM((4, tok, width), BF16),
            pltpu.VMEM((tok // 2, width), BF16),
            pltpu.VMEM((tok // 2, width), BF16),
            pltpu.VMEM((tok, width), BF16),
            pltpu.VMEM((tok, width), BF16),
            pltpu.VMEM((tok, width), BF16),
            pltpu.SemaphoreType.DMA((MAX_SEMS,)),
            pltpu.SemaphoreType.DMA((MAX_SEMS,)),
            pltpu.SemaphoreType.DMA((4 + len(PARTS),)),
        ],
        compiler_params=pltpu.CompilerParams(
            collective_id=0, has_side_effects=True, vmem_limit_bytes=60 * 1024 * 1024
        ),
        name="routed_experts",
    )(tokens, expert_ids.T, gate_probs.T, w_gate, w_up, w_down)


def solution(mesh):
    placed = (
        P(("dp", "ep"), None),
        P(("dp", "ep"), None),
        P(("dp", "ep"), None),
        P("ep", None, None),
        P("ep", None, None),
        P("ep", None, None),
    )
    return jax.shard_map(
        functools.partial(shards, mesh.shape["dp"] // 2), mesh=mesh, in_specs=placed,
        out_specs=P(("dp", "ep"), None), check_vma=False,
    )
```

time: 180 us -> 83.7 us (0.47)
  Pallas kernels: 0 us -> 81.9 us
  blocking collectives: 61.3 us -> 0 us
  waiting for transfers between devices: 57.1 us -> 0 us
  local copies, waits for them, and re-layouts: 23.5 us -> 1.67 us
  matrix products: 19.8 us -> 0 us
  starting transfers between devices: 12.3 us -> 0 us
  other arithmetic: 4.6 us -> 0 us
    pallas_call x0 -> x1, Pallas kernels: none -> 81.9 us  [shards(): pl.pallas_call(functools.partial(kernel, (n_hi, tok, width, hid, most)),...]
    all_to_all x1 -> x0, blocking collectives: 61.3 us -> none  [shards(): lax.all_to_all(send_rows, 'ep', split_axis=0, concat_axis=0, tiled=True)]
    all_to_all x1 -> x0, waiting for transfers between devices: 57.1 us -> none  [shards(): lax.all_to_all(served, 'ep', split_axis=0, concat_axis=0, tiled=True)]
    dot_general x3 -> x0, matrix products: 19.8 us -> none  [the longest x1 12.3 us: expert_ffn(): jnp.dot(hidden, down_matrix, preferred_element_type=jnp.float32)]
    gather x2 -> x0, local copies, waits for them, and re-layouts: 14 us -> none  [the longest x1 8.02 us: shards(): gathered.reshape(-1, features)[slot_index]]
    all_to_all x1 -> x0, starting transfers between devices: 12.3 us -> none  [shards(): lax.all_to_all(served, 'ep', split_axis=0, concat_axis=0, tiled=True)]
    scatter x2 -> x0, local copies, waits for them, and re-layouts: 4.89 us -> none  [the longest x1 2.45 us: shards(): filled = jnp.zeros((ep_count * most,), jnp.bool_).at[slot_index].set(True)]
    select_n x3 -> x0, other arithmetic: 2.55 us -> none  [the longest x1 2.54 us: shards(): jnp.where(filled[:, None], tokens[slot_token], jnp.zeros((), jnp.bfloat16))]
  transfers between devices with their start and end apart: 1 -> 0, of which waited for: 1 -> 0; matrix products, arithmetic and copies ran while one was open for 0% -> 0% of each run, Pallas kernels for 0% -> 0%
where the time goes in v2:
time: 83.7 us; the launch traced here: 83.6 us
  Pallas kernels  81.9 us (98%)
  local copies, waits for them, and re-layouts  1.67 us (2%)
    pallas_call x1, Pallas kernels, shards(): pl.pallas_call(functools.partial(kernel, (n_hi, tok, width, hid, most)),...  81.9 us

profile of v2, /device:TPU:1, one launch (start us, length us, event | category | flops | bytes accessed | tf_op | source)
XLA Modules:
  0.0 83.6 jit_solution(12492562940243291070)
XLA Ops:
  0.0 81.9 %routed_experts.1 = bf16[64,2048]{1,0:T(8,128)(2,1)} custom-call(bf16[64,2048]{1,0:T(8,128)(2,1)} %tok_hbm.1, s32[8,64]{1,0:T(8,128)} %bitcast.2, f32[8,64]{1,0:T(8,128)} %bitcast.3, bf16[1,2048,768]{2,1,0:T(8,128)(2,1)} %wg_hbm.1, bf16[1,2048,768]{2,1,0:T(8,128)(2,1)} %wu_hbm.1, bf16[1,768,2048]{2,1,0:T(8,128)(2,1)} %wd_hbm.1), custom_call_target="tpu_custom_call" | custom-call | tf_op jit(solution)/shard_map/routed_experts/pallas_call | solution.py:413
  81.9 1.7 %copy.8 = bf16[64,2048]{1,0:T(8,128)(2,1)} copy(bf16[64,2048]{1,0:T(8,128)(2,1)} %routed_experts.1) | data formatting | bytes 524288

commit v3 on v2

--- a/solution.py
+++ b/solution.py
@@ -11,22 +11,23 @@
 F32, BF16 = jnp.float32, jnp.bfloat16
 OPPOSITE = {"xp": "xm", "xm": "xp", "yp": "ym", "ym": "yp", "zp": "zm", "zm": "zp"}
 
-ORDER = [
-    (0, 0), (1, 0), (3, 0), (0, 1), (0, 3), (1, 1), (1, 3), (3, 1),
-    (3, 3), (0, 2), (2, 0), (1, 2), (3, 2), (2, 1), (2, 3), (2, 2),
-]
-PLACE = {slot: place for place, slot in enumerate(ORDER)}
-PARTS = (2, 2, 2, 1, 1)
+CLUSTER = [(0, 0), (1, 0), (3, 0), (0, 1), (0, 3)]
+OTHERS = [(1, 1), (3, 3), (1, 3), (3, 1), (0, 2), (2, 0), (1, 2), (2, 1), (3, 2), (2, 3), (2, 2)]
+PLACE = {slot: place for place, slot in enumerate(CLUSTER + [None] + OTHERS) if slot}
+PLACES = 18
+NEAR = {1: "xp", 2: "xm", 3: "yp", 4: "ym"}
+PARTS = (1, 1, 2, 2, 1, 1)
 STEPS = (
-    "E0", "E1", "A0", "A1", "E2", "B0", "B1", "E3", "A2", "E4", "C0", "C1", "A3", "B2", "A4", "D0", "D1", "B3", "C2", "B4",
-    "C3", "D2", "C4", "D3", "D4",
+    "E0", "E1", "A0", "F0", "A1", "E2", "B0", "B1", "A2", "E3", "C0", "C1", "E4", "B2", "E5", "A3", "D0", "D1", "A4", "C2", "A5",
+    "B3", "B4", "D2", "B5", "C3", "C4", "C5", "D3", "D4", "D5",
 )
-MAX_SEMS = 64
+MAX_SEMS = 96
 
 
 def kernel(
     sizes, tok_hbm, ids_ref, probs_ref, wg_hbm, wu_hbm, wd_hbm, out_hbm,
     gath, meta, comb, xown, zsend, zrecv, hown, hz, wg, wu, wd, zout, both, part, picks,
+    fgath, fmeta, fcomb, fpick, fsend, frecv, fsum, zsum,
     r1p, r1m, r2p, r2m, r4p, r4m, r5p, r5m, outv,
     send_sem, recv_sem, local_sem,
 ):
@@ -130,10 +131,11 @@
         move("far", "pass", "ym", (0, 1), quarters[3])
 
     def passes(d):
-        move(f"pass{d}", "pass", "yp", (d, 0), first, "m12")
+        e = (4 - d) % 4
         move(f"pass{d}", "pass", "ym", (d, 0), first, "m12")
-        move(f"pass{d}", "second", "xp", (0, d), second)
         move(f"pass{d}", "second", "xm", (0, d), second)
+        move(f"pass{d}", "pass", "yp", (e, 0), first, "m12")
+        move(f"pass{d}", "second", "xp", (0, e), second)
 
     def relays(d):
         move(f"relay{d}", "relay", "yp", (d, 3), quarters[0], "m12" if d else None)
@@ -172,28 +174,72 @@
         comb[place] = scaled.T.astype(BF16)
         picks[place] = one.astype(BF16)
 
-    def select(dx, dy, side):
+    def select(dx, dy):
         place = PLACE[dx, dy]
-
-        @pl.loop(0, 2)
+        rows = most if place < 5 else 2 * most
+
+        @pl.loop(0, 4)
         def _(q):
-            cols = pl.ds(pl.multiple_of(side * half + q * quarter, quarter), quarter)
-            rows = jnp.dot(picks[place], gath[dx, dy, :, cols], preferred_element_type=F32).astype(BF16)
-            xown[place, :, cols] = rows[:most]
-            zsend[place, :, cols] = rows[most:]
-
-        cols = (first, second)[side]
-        way = "zm" if place % 2 else "zp"
-        send(way, zsend.at[place, :, cols], zrecv.at[place, :, cols], "rows", f"rows{place // 4}")
+            cols = pl.ds(pl.multiple_of(q * quarter, quarter), quarter)
+            chosen = jnp.dot(picks[place, :rows], gath[dx, dy, :, cols], preferred_element_type=F32).astype(BF16)
+            xown[place, :, cols] = chosen[:most]
+            if place >= 5:
+                zsend[place, :, cols] = chosen[most:]
+
+        if place >= 5:
+            group = min((place - 6) // 4, 2)
+            send("zm" if place % 2 else "zp", zsend.at[place], zrecv.at[place], "rows", f"rows{group}")
 
     def select_all(*slots):
         for slot in slots:
             build(*slot)
-            select(*slot, 0)
-            select(*slot, 1)
+            select(*slot)
 
     def got_rows(group):
-        wait(f"rows{group}", zrecv.at[pl.ds(4 * group, 4)])
+        wait(f"rows{group}", zrecv.at[pl.ds(0, (4, 4, 3)[group])])
+
+    near_experts = (ep, at(lax.rem(x + 1, 4), y, z_lo), at(lax.rem(x + 3, 4), y, z_lo), at(x, lax.rem(y + 1, 4), z_lo), at(x, lax.rem(y + 3, 4), z_lo))
+
+    def select_foreign():
+        for i, expert in enumerate(near_experts):
+            row = (expert * most + lax.broadcasted_iota(jnp.int32, (most, tok), 0)).astype(F32)
+            one, scaled = jnp.zeros((most, tok), F32), jnp.zeros((most, tok), F32)
+            for k in range(8):
+                hit = fmeta[k:k + 1, 0:tok] == row
+                one = one + jnp.where(hit, 1.0, 0.0)
+                scaled = scaled + jnp.where(hit, fmeta[8 + k:9 + k, 0:tok], 0.0)
+            fcomb[i] = scaled.T.astype(BF16)
+            fpick[i * most:(i + 1) * most, :] = one.astype(BF16)
+
+        @pl.loop(0, 4)
+        def _(q):
+            cols = pl.ds(pl.multiple_of(q * quarter, quarter), quarter)
+            chosen = jnp.dot(fpick[...], fgath[:, cols], preferred_element_type=F32).astype(BF16)
+            zrecv[0, :, cols] = chosen[:most]
+            for i in range(4):
+                fsend[i, :, cols] = chosen[(i + 1) * most:(i + 2) * most]
+
+    def send_near():
+        for i, (way, slot) in enumerate((("xp", (3, 0)), ("xm", (1, 0)), ("yp", (0, 3)), ("ym", (0, 1)))):
+            send(way, fsend.at[i], zrecv.at[PLACE[slot]], "near", "near")
+
+    def back_near():
+        for place, way in NEAR.items():
+            index = ("xm", "xp", "ym", "yp").index(way)
+            send(way, zout.at[place // 2, place % 2], frecv.at[index], "nearback", "nearback")
+
+    def sum_near():
+        wait("nearback", frecv)
+
+        @pl.loop(0, 4)
+        def _(q):
+            cols = pl.ds(pl.multiple_of(q * quarter, quarter), quarter)
+            total = jnp.dot(fcomb[0], zout[0, 0, :, cols], preferred_element_type=F32)
+            for i in range(4):
+                total = total + jnp.dot(fcomb[i + 1], frecv[i, :, cols], preferred_element_type=F32)
+            fsum[:, cols] = total.astype(BF16)
+
+        send("zp", fsum, zsum, "sum", "sum")
 
     tile = 256
 
@@ -210,39 +256,45 @@
 
     own_first()
     own_second()
+    send("zm", gath.at[0, 0], fgath, "whole", "whole")
+    send("zm", meta.at[0, 0], fmeta, "mwhole", "mwhole")
     select_all((0, 0))
     got_own()
+    passes(1)
     own_relay()
-    passes(1)
     passes(3)
-    for slot in ORDER[1:5]:
+    for slot in CLUSTER[1:]:
         build(*slot)
-        select(*slot, 0 if slot[1] == 0 else 1)
     got_passes(0)
     relays(0)
-    for slot in ORDER[1:5]:
-        select(*slot, 1 if slot[1] == 0 else 0)
+    for slot in CLUSTER[1:]:
+        select(*slot)
+    wait("whole", fgath)
+    wait("mwhole", fmeta)
+    select_foreign()
+    loads[0].wait()
+    loads[1].wait()
+    gate_up(xown, hown, 0, 5, 0, 2)
+    got_passes(1)
+    select_all((1, 1), (3, 3))
     got_far()
     passes(2)
-    got_passes(1)
+    gate_up(xown, hown, 0, 5, 2, 3)
+    got_passes(3)
     relays(1)
-    select_all((1, 1))
-    got_passes(3)
     relays(3)
-    select_all((1, 3), (3, 1), (3, 3))
+    select_all((1, 3), (3, 1))
     got_relays(0)
     select_all((0, 2), (2, 0))
-    loads[0].wait()
-    loads[1].wait()
-    gate_up(xown, hown, 0, 8, 0, 1)
+    gate_up(xown, hown, 6, 6, 0, 1)
     got_passes(2)
     relays(2)
-    gate_up(xown, hown, 0, 8, 1, 2)
+    send_near()
+    gate_up(xown, hown, 6, 6, 1, 2)
     got_relays(1)
     select_all((1, 2), (2, 1))
     got_relays(3)
     select_all((3, 2), (2, 3))
-    gate_up(xown, hown, 0, 8, 2, 3)
     got_relays(2)
     select_all((2, 2))
 
@@ -257,62 +309,80 @@
 
     top, low = pl.ds(0, tok // 2), pl.ds(tok // 2, tok // 2)
 
-    def down_z(group, c):
-        rows = 8 * most
-        out = jnp.dot(hz[rows * group:rows * (group + 1), :], wd[:, chunk_cols(c)], preferred_element_type=F32)
-        zout[4 * group:4 * group + 4, :, :, chunk_cols(c)] = out.astype(BF16).reshape(4, 2, most, chunk_cols(c).size)
+    def down_z(part_of, c):
+        place, places = ((6, 8), (14, 3))[part_of]
+        cols = chunk_cols(c)
+        out = jnp.dot(hz[most * place:most * (place + places), :], wd[:, cols], preferred_element_type=F32).astype(BF16)
+        for i in range(places):
+            zout[(place + i) // 2, (place + i) % 2, :, cols] = out[most * i:most * (i + 1)]
         for side, way in ((0, "zm"), (1, "zp")):
+            pairs = pl.ds(place // 2, (places + 1 - side) // 2)
             send(
                 way,
-                zout.at[pl.ds(4 * group, 4), side, :, chunk_cols(c)],
-                both.at[pl.ds(4 * group, 4), side, pl.ds(most, most), chunk_cols(c)],
+                zout.at[pairs, side, :, cols],
+                both.at[pairs, side, pl.ds(most, most), cols],
                 "back", f"back{c}",
             )
 
+    def down_near():
+        @pl.loop(0, 4)
+        def _(q):
+            cols = pl.ds(pl.multiple_of(q * quarter, quarter), quarter)
+            out = jnp.dot(hz[0:5 * most, :], wd[:, cols], preferred_element_type=F32).astype(BF16)
+            for i in range(5):
+                zout[i // 2, i % 2, :, cols] = out[most * i:most * (i + 1)]
+
+        back_near()
+
     def down_own(c):
-        out = jnp.dot(hown[...], wd[:, chunk_cols(c)], preferred_element_type=F32)
-        both[:, :, 0:most, chunk_cols(c)] = out.astype(BF16).reshape(8, 2, most, chunk_cols(c).size)
-
+        cols = chunk_cols(c)
+        out = jnp.dot(hown[...], wd[:, cols], preferred_element_type=F32).astype(BF16)
+        for slot, place in PLACE.items():
+            both[place // 2, place % 2, 0:most, cols] = out[most * place:most * (place + 1)]
+
+    gate_up(xown, hown, 6, 6, 2, 3)
+    gate_up(xown, hown, 12, 5)
     got_rows(0)
     got_rows(1)
-    gate_up(zrecv, hz, 0, 8)
+    gate_up(zrecv, hz, 6, 8)
     loads[2].wait()
     down_z(0, 0)
     down_z(0, 1)
-    gate_up(xown, hown, 8, 8)
+    wait("near", zrecv.at[pl.ds(0, 4)])
+    gate_up(zrecv, hz, 0, 5)
     got_rows(2)
-    gate_up(zrecv, hz, 8, 4)
-    down_own(0)
-    down_own(1)
-    got_rows(3)
-    gate_up(zrecv, hz, 12, 4)
+    gate_up(zrecv, hz, 14, 3)
     down_z(1, 0)
     down_z(1, 1)
     for c in range(2, len(PARTS)):
         down_z(0, c)
         down_z(1, c)
+    down_near()
+    down_own(0)
+    down_own(1)
 
     def expand(c):
         cols = chunk_cols(c)
         left, right = sides(c)
         if c >= 2:
             down_own(c)
-        wait(f"back{c}", zout.at[:, :, :, cols])
+        wait(f"back{c}", zrecv.at[pl.ds(0, 11), :, cols])
 
         def fill(dx, dy):
             place = PLACE[dx, dy]
+            rows = most if place < 5 else 2 * most
             part[dx, dy, :, cols] = jnp.dot(
-                comb[place], both[place // 2, place % 2, :, cols], preferred_element_type=F32
+                comb[place, :, :rows], both[place // 2, place % 2, :rows, cols], preferred_element_type=F32
             ).astype(BF16)
 
-        far = [slot for slot in ORDER if 2 in slot]
+        far = [slot for slot in PLACE if 2 in slot]
         for slot in far:
             fill(*slot)
         send("yp", part.at[:, 2, top, left], r1p.at[:, :, left], "1p", f"1{c}")
         send("ym", part.at[:, 2, low, left], r1m.at[:, :, left], "1m", f"1{c}")
         send("xp", part.at[2, :, top, right], r1p.at[:, :, right], "1p", f"1{c}")
         send("xm", part.at[2, :, low, right], r1m.at[:, :, right], "1m", f"1{c}")
-        for slot in ORDER:
+        for slot in PLACE:
             if slot not in far:
                 fill(*slot)
         halves_two(c, low, top)
@@ -379,25 +449,33 @@
 
     def step_five(c):
         wait(f"5{c}", r5p.at[:, double(c)])
+        if c == 0:
+            wait("sum", zsum)
         for cols in sides(c):
-            total = part[0, 0, :, cols].astype(F32) + r5p[:, cols].astype(F32) + r5m[:, cols].astype(F32)
+            total = part[0, 0, :, cols].astype(F32) + zsum[:, cols].astype(F32) + r5p[:, cols].astype(F32) + r5m[:, cols].astype(F32)
             outv[:, cols] = total.astype(BF16)
         cols = chunk_cols(c)
         store = pltpu.make_async_copy(outv.at[:, cols], out_hbm.at[:, cols], local_sem.at[4 + c])
         store.start()
         stores.append(store)
 
-    run = {"E": expand, "A": step_two, "B": step_three, "C": step_four, "D": step_five}
+    run = {"E": expand, "A": step_two, "B": step_three, "C": step_four, "D": step_five, "F": lambda c: sum_near()}
     for step in STEPS:
         run[step[0]](int(step[1]))
+    assert len(sems) <= MAX_SEMS
     drain("own", gath.at[0])
     drain("pass", gath.at[0])
     drain("second", gath.at[0, 0:3])
     drain("relay", gath.at[0])
     drain("m12", meta.at[0:3])
     drain("m3", meta.at[0, 0:3])
-    drain("rows", zsend)
-    drain("back", zout)
+    drain("rows", zsend.at[pl.ds(0, 11)])
+    drain("back", zsend.at[pl.ds(0, 11)])
+    drain("near", frecv)
+    drain("nearback", frecv)
+    drain("whole", fgath)
+    drain("mwhole", fmeta)
+    drain("sum", fsum)
     for kind, like in (("1p", r1p), ("1m", r1m), ("2p", r2p), ("2m", r2m), ("4p", r4p), ("4m", r4m), ("5p", r5p), ("5m", r5m)):
         drain(kind, like)
     for store in stores:
@@ -418,19 +496,27 @@
         scratch_shapes=[
             pltpu.VMEM((4, 4, tok, width), BF16),
             pltpu.VMEM((4, 4, 16, 128), F32),
-            pltpu.VMEM((16, tok, 2 * most), BF16),
-            pltpu.VMEM((16, most, width), BF16),
-            pltpu.VMEM((16, most, width), BF16),
-            pltpu.VMEM((16, most, width), BF16),
-            pltpu.VMEM((16 * most, hid), BF16),
-            pltpu.VMEM((16 * most, hid), BF16),
+            pltpu.VMEM((PLACES, tok, 2 * most), BF16),
+            pltpu.VMEM((PLACES, most, width), BF16),
+            pltpu.VMEM((PLACES, most, width), BF16),
+            pltpu.VMEM((PLACES, most, width), BF16),
+            pltpu.VMEM((PLACES * most, hid), BF16),
+            pltpu.VMEM((PLACES * most, hid), BF16),
             pltpu.VMEM((width, hid), BF16),
             pltpu.VMEM((width, hid), BF16),
             pltpu.VMEM((hid, width), BF16),
-            pltpu.VMEM((8, 2, most, width), BF16),
-            pltpu.VMEM((8, 2, 2 * most, width), BF16),
+            pltpu.VMEM((PLACES // 2, 2, most, width), BF16),
+            pltpu.VMEM((PLACES // 2, 2, 2 * most, width), BF16),
             pltpu.VMEM((4, 4, tok, width), BF16),
-            pltpu.VMEM((16, 2 * most, tok), BF16),
+            pltpu.VMEM((PLACES, 2 * most, tok), BF16),
+            pltpu.VMEM((tok, width), BF16),
+            pltpu.VMEM((16, 128), F32),
+            pltpu.VMEM((5, tok, most), BF16),
+            pltpu.VMEM((5 * most, tok), BF16),
+            pltpu.VMEM((4, most, width), BF16),
+            pltpu.VMEM((4, most, width), BF16),
+            pltpu.VMEM((tok, width), BF16),
+            pltpu.VMEM((tok, width), BF16),
             pltpu.VMEM((4, tok // 2, width), BF16),
             pltpu.VMEM((4, tok // 2, width), BF16),
             pltpu.VMEM((4, tok, width), BF16),

time: 83.7 us -> 86.6 us (1.035)
  Pallas kernels: 81.9 us -> 84.8 us
    pallas_call x1, Pallas kernels: 81.9 us -> 84.8 us  [shards(): pl.pallas_call(functools.partial(kernel, (n_hi, tok, width, hid, most)),...]
where the time goes in v3:
time: 86.6 us; the launch traced here: 86.5 us
  Pallas kernels  84.8 us (98%)
  local copies, waits for them, and re-layouts  1.67 us (2%)
    pallas_call x1, Pallas kernels, shards(): pl.pallas_call(functools.partial(kernel, (n_hi, tok, width, hid, most)),...  84.8 us

profile of v3, /device:TPU:1, one launch (start us, length us, event | category | flops | bytes accessed | tf_op | source)
XLA Modules:
  0.0 86.5 jit_solution(12702043061516554657)
XLA Ops:
  0.0 84.8 %routed_experts.1 = bf16[64,2048]{1,0:T(8,128)(2,1)} custom-call(bf16[64,2048]{1,0:T(8,128)(2,1)} %tok_hbm.1, s32[8,64]{1,0:T(8,128)} %bitcast.2, f32[8,64]{1,0:T(8,128)} %bitcast.3, bf16[1,2048,768]{2,1,0:T(8,128)(2,1)} %wg_hbm.1, bf16[1,2048,768]{2,1,0:T(8,128)(2,1)} %wu_hbm.1, bf16[1,768,2048]{2,1,0:T(8,128)(2,1)} %wd_hbm.1), custom_call_target="tpu_custom_call" | custom-call | tf_op jit(solution)/shard_map/routed_experts/pallas_call | solution.py:491
  84.8 1.7 %copy.8 = bf16[64,2048]{1,0:T(8,128)(2,1)} copy(bf16[64,2048]{1,0:T(8,128)(2,1)} %routed_experts.1) | data formatting | bytes 524288

commit v4 on v3

--- a/solution.py
+++ b/solution.py
@@ -18,8 +18,8 @@
 NEAR = {1: "xp", 2: "xm", 3: "yp", 4: "ym"}
 PARTS = (1, 1, 2, 2, 1, 1)
 STEPS = (
-    "E0", "E1", "A0", "F0", "A1", "E2", "B0", "B1", "A2", "E3", "C0", "C1", "E4", "B2", "E5", "A3", "D0", "D1", "A4", "C2", "A5",
-    "B3", "B4", "D2", "B5", "C3", "C4", "C5", "D3", "D4", "D5",
+    "G0", "G1", "Z0", "W1", "G2", "F0", "W2", "E0", "G3", "E1", "E2", "A0", "W3", "G4", "E3", "A1", "A2", "G5", "B0", "E4", "E5",
+    "A3", "B1", "B2", "C0", "A4", "A5", "B3", "C1", "C2", "D0", "B4", "B5", "C3", "D1", "D2", "C4", "C5", "D3", "D4", "D5",
 )
 MAX_SEMS = 96
 
@@ -290,7 +290,7 @@
     got_passes(2)
     relays(2)
     send_near()
-    gate_up(xown, hown, 6, 6, 1, 2)
+    gate_up(xown, hown, 6, 6, 1, 3)
     got_relays(1)
     select_all((1, 2), (2, 1))
     got_relays(3)
@@ -309,20 +309,24 @@
 
     top, low = pl.ds(0, tok // 2), pl.ds(tok // 2, tok // 2)
 
-    def down_z(part_of, c):
+    def quarter_chunks(q):
+        return [c for c in range(len(PARTS)) if q * quarter <= starts[c] < (q + 1) * quarter]
+
+    def down_z(part_of, q):
         place, places = ((6, 8), (14, 3))[part_of]
-        cols = chunk_cols(c)
-        out = jnp.dot(hz[most * place:most * (place + places), :], wd[:, cols], preferred_element_type=F32).astype(BF16)
+        rows = hz[most * place:most * (place + places), :]
+        out = jnp.dot(rows, wd[:, quarters[q]], preferred_element_type=F32).astype(BF16)
         for i in range(places):
-            zout[(place + i) // 2, (place + i) % 2, :, cols] = out[most * i:most * (i + 1)]
-        for side, way in ((0, "zm"), (1, "zp")):
-            pairs = pl.ds(place // 2, (places + 1 - side) // 2)
-            send(
-                way,
-                zout.at[pairs, side, :, cols],
-                both.at[pairs, side, pl.ds(most, most), cols],
-                "back", f"back{c}",
-            )
+            zout[(place + i) // 2, (place + i) % 2, :, quarters[q]] = out[most * i:most * (i + 1)]
+        for c in quarter_chunks(q):
+            for side, way in ((0, "zm"), (1, "zp")):
+                pairs = pl.ds(place // 2, (places + 1 - side) // 2)
+                send(
+                    way,
+                    zout.at[pairs, side, :, chunk_cols(c)],
+                    both.at[pairs, side, pl.ds(most, most), chunk_cols(c)],
+                    "back", f"back{part_of}{c}",
+                )
 
     def down_near():
         @pl.loop(0, 4)
@@ -334,13 +338,11 @@
 
         back_near()
 
-    def down_own(c):
-        cols = chunk_cols(c)
-        out = jnp.dot(hown[...], wd[:, cols], preferred_element_type=F32).astype(BF16)
-        for slot, place in PLACE.items():
-            both[place // 2, place % 2, 0:most, cols] = out[most * place:most * (place + 1)]
-
-    gate_up(xown, hown, 6, 6, 2, 3)
+    def down_own(q):
+        out = jnp.dot(hown[...], wd[:, quarters[q]], preferred_element_type=F32).astype(BF16)
+        for place in PLACE.values():
+            both[place // 2, place % 2, 0:most, quarters[q]] = out[most * place:most * (place + 1)]
+
     gate_up(xown, hown, 12, 5)
     got_rows(0)
     got_rows(1)
@@ -348,44 +350,57 @@
     loads[2].wait()
     down_z(0, 0)
     down_z(0, 1)
+    down_z(0, 2)
     wait("near", zrecv.at[pl.ds(0, 4)])
     gate_up(zrecv, hz, 0, 5)
+    down_near()
     got_rows(2)
     gate_up(zrecv, hz, 14, 3)
     down_z(1, 0)
     down_z(1, 1)
-    for c in range(2, len(PARTS)):
-        down_z(0, c)
-        down_z(1, c)
-    down_near()
     down_own(0)
-    down_own(1)
-
-    def expand(c):
+
+    def down_rest(c):
+        down_z(0, 3)
+        down_z(1, 2)
+        down_z(1, 3)
+
+    def fill(c, *slots):
         cols = chunk_cols(c)
-        left, right = sides(c)
-        if c >= 2:
-            down_own(c)
-        wait(f"back{c}", zrecv.at[pl.ds(0, 11), :, cols])
-
-        def fill(dx, dy):
+        for dx, dy in slots:
             place = PLACE[dx, dy]
             rows = most if place < 5 else 2 * most
             part[dx, dy, :, cols] = jnp.dot(
                 comb[place, :, :rows], both[place // 2, place % 2, :rows, cols], preferred_element_type=F32
             ).astype(BF16)
 
-        far = [slot for slot in PLACE if 2 in slot]
-        for slot in far:
-            fill(*slot)
-        send("yp", part.at[:, 2, top, left], r1p.at[:, :, left], "1p", f"1{c}")
-        send("ym", part.at[:, 2, low, left], r1m.at[:, :, left], "1m", f"1{c}")
-        send("xp", part.at[2, :, top, right], r1p.at[:, :, right], "1p", f"1{c}")
-        send("xm", part.at[2, :, low, right], r1m.at[:, :, right], "1m", f"1{c}")
-        for slot in PLACE:
-            if slot not in far:
-                fill(*slot)
-        halves_two(c, low, top)
+    late = ((3, 2), (2, 3), (2, 2))
+
+    def halves_one(c, pair):
+        left, right = sides(c)
+        send("yp", part.at[pair, 2, top, left], r1p.at[pair, :, left], "1p", f"1{c}")
+        send("ym", part.at[pair, 2, low, left], r1m.at[pair, :, left], "1m", f"1{c}")
+        send("xp", part.at[2, pair, top, right], r1p.at[pair, :, right], "1p", f"1{c}")
+        send("xm", part.at[2, pair, low, right], r1m.at[pair, :, right], "1m", f"1{c}")
+
+    def expand(c):
+        left, right = sides(c)
+        wait(f"back0{c}", zrecv.at[pl.ds(0, 8), :, chunk_cols(c)])
+        fill(c, (0, 2), (1, 2), (2, 0), (2, 1))
+        halves_one(c, pl.ds(0, 2))
+        fill(c, *[slot for slot in PLACE if 2 not in slot])
+        send("yp", part.at[:, 1, low, left], r2p.at[:, low, left], "2p", f"2{c}")
+        send("xp", part.at[1, :, low, right], r2p.at[:, low, right], "2p", f"2{c}")
+        send("ym", part.at[pl.ds(0, 2), 3, top, left], r2m.at[pl.ds(0, 2), top, left], "2m", f"2{c}")
+        send("xm", part.at[3, pl.ds(0, 2), top, right], r2m.at[pl.ds(0, 2), top, right], "2m", f"2{c}")
+
+    def expand_late(c):
+        left, right = sides(c)
+        wait(f"back1{c}", zrecv.at[pl.ds(0, 3), :, chunk_cols(c)])
+        fill(c, *late)
+        halves_one(c, pl.ds(2, 2))
+        send("ym", part.at[pl.ds(2, 2), 3, top, left], r2m.at[pl.ds(2, 2), top, left], "2m", f"2{c}")
+        send("xm", part.at[3, pl.ds(2, 2), top, right], r2m.at[pl.ds(2, 2), top, right], "2m", f"2{c}")
 
     def halves_two(c, plus, minus):
         left, right = sides(c)
@@ -459,7 +474,7 @@
         store.start()
         stores.append(store)
 
-    run = {"E": expand, "A": step_two, "B": step_three, "C": step_four, "D": step_five, "F": lambda c: sum_near()}
+    run = {"G": expand, "E": expand_late, "Z": down_rest, "W": down_own, "A": step_two, "B": step_three, "C": step_four, "D": step_five, "F": lambda c: sum_near()}
     for step in STEPS:
         run[step[0]](int(step[1]))
     assert len(sems) <= MAX_SEMS

time: 86.6 us -> 81.3 us (0.939)
  Pallas kernels: 84.8 us -> 79.5 us
    pallas_call x1, Pallas kernels: 84.8 us -> 79.5 us  [shards(): pl.pallas_call(functools.partial(kernel, (n_hi, tok, width, hid, most)),...]
where the time goes in v4:
time: 81.3 us; the launch traced here: 81.1 us
  Pallas kernels  79.5 us (98%)
  local copies, waits for them, and re-layouts  1.67 us (2%)
    pallas_call x1, Pallas kernels, shards(): pl.pallas_call(functools.partial(kernel, (n_hi, tok, width, hid, most)),...  79.5 us
    unnamed x1, local copies, waits for them, and re-layouts  1.67 us

profile of v4, /device:TPU:1, one launch (start us, length us, event | category | flops | bytes accessed | tf_op | source)
XLA Modules:
  0.0 81.1 jit_solution(11561837031713456547)
XLA Ops:
  0.0 79.5 %routed_experts.1 = bf16[64,2048]{1,0:T(8,128)(2,1)} custom-call(bf16[64,2048]{1,0:T(8,128)(2,1)} %tok_hbm.1, s32[8,64]{1,0:T(8,128)} %bitcast.2, f32[8,64]{1,0:T(8,128)} %bitcast.3, bf16[1,2048,768]{2,1,0:T(8,128)(2,1)} %wg_hbm.1, bf16[1,2048,768]{2,1,0:T(8,128)(2,1)} %wu_hbm.1, bf16[1,768,2048]{2,1,0:T(8,128)(2,1)} %wd_hbm.1), custom_call_target="tpu_custom_call" | custom-call | tf_op jit(solution)/shard_map/routed_experts/pallas_call | solution.py:506
  79.5 1.7 %copy.8 = bf16[64,2048]{1,0:T(8,128)(2,1)} copy(bf16[64,2048]{1,0:T(8,128)(2,1)} %routed_experts.1) | data formatting | bytes 524288

commit v5 on v4

--- a/solution.py
+++ b/solution.py
@@ -16,12 +16,14 @@
 PLACE = {slot: place for place, slot in enumerate(CLUSTER + [None] + OTHERS) if slot}
 PLACES = 18
 NEAR = {1: "xp", 2: "xm", 3: "yp", 4: "ym"}
-PARTS = (1, 1, 2, 2, 1, 1)
+PARTS = (1,) * 8
 STEPS = (
-    "G0", "G1", "Z0", "W1", "G2", "F0", "W2", "E0", "G3", "E1", "E2", "A0", "W3", "G4", "E3", "A1", "A2", "G5", "B0", "E4", "E5",
-    "A3", "B1", "B2", "C0", "A4", "A5", "B3", "C1", "C2", "D0", "B4", "B5", "C3", "D1", "D2", "C4", "C5", "D3", "D4", "D5",
+    "O3", "W2", "Z", "a2", "a3", "N", "L", "DN", "b2", "G4", "b3", "W3", "G5", "W0", "a0", "b0", "W1", "G6", "E4",
+    "E5", "a1", "G7", "E7", "b1", "E6", "G0", "A4", "A5", "E0", "G1", "F", "E1", "B4", "G2", "G3", "E2", "E3", "A7",
+    "A0", "A6", "A2", "A3", "A1", "C4", "B7", "B5", "B6", "B2", "B0", "B3", "B1", "D4", "C5", "C6", "C7", "C2", "C0",
+    "C3", "C1", "D5", "D7", "D3", "D6", "D2", "D0", "D1",
 )
-MAX_SEMS = 96
+MAX_SEMS = 128
 
 
 def kernel(
@@ -178,7 +180,7 @@
         place = PLACE[dx, dy]
         rows = most if place < 5 else 2 * most
 
-        @pl.loop(0, 4)
+        @pl.loop(0, 4, unroll=4)
         def _(q):
             cols = pl.ds(pl.multiple_of(q * quarter, quarter), quarter)
             chosen = jnp.dot(picks[place, :rows], gath[dx, dy, :, cols], preferred_element_type=F32).astype(BF16)
@@ -211,7 +213,7 @@
             fcomb[i] = scaled.T.astype(BF16)
             fpick[i * most:(i + 1) * most, :] = one.astype(BF16)
 
-        @pl.loop(0, 4)
+        @pl.loop(0, 4, unroll=4)
         def _(q):
             cols = pl.ds(pl.multiple_of(q * quarter, quarter), quarter)
             chosen = jnp.dot(fpick[...], fgath[:, cols], preferred_element_type=F32).astype(BF16)
@@ -231,7 +233,7 @@
     def sum_near():
         wait("nearback", frecv)
 
-        @pl.loop(0, 4)
+        @pl.loop(0, 4, unroll=4)
         def _(q):
             cols = pl.ds(pl.multiple_of(q * quarter, quarter), quarter)
             total = jnp.dot(fcomb[0], zout[0, 0, :, cols], preferred_element_type=F32)
@@ -246,7 +248,7 @@
     def gate_up(rows_ref, hidden, place, places, start=0, stop=hid // tile):
         rows = places * most
 
-        @pl.loop(start, stop)
+        @pl.loop(start, stop, unroll=stop - start)
         def _(n):
             cols = pl.ds(pl.multiple_of(n * tile, tile), tile)
             block = rows_ref[place:place + places].reshape(rows, width)
@@ -272,8 +274,8 @@
     wait("whole", fgath)
     wait("mwhole", fmeta)
     select_foreign()
-    loads[0].wait()
-    loads[1].wait()
+    for load in loads:
+        load.wait()
     gate_up(xown, hown, 0, 5, 0, 2)
     got_passes(1)
     select_all((1, 1), (3, 3))
@@ -329,7 +331,7 @@
                 )
 
     def down_near():
-        @pl.loop(0, 4)
+        @pl.loop(0, 4, unroll=4)
         def _(q):
             cols = pl.ds(pl.multiple_of(q * quarter, quarter), quarter)
             out = jnp.dot(hz[0:5 * most, :], wd[:, cols], preferred_element_type=F32).astype(BF16)
@@ -343,27 +345,21 @@
         for place in PLACE.values():
             both[place // 2, place % 2, 0:most, quarters[q]] = out[most * place:most * (place + 1)]
 
-    gate_up(xown, hown, 12, 5)
-    got_rows(0)
-    got_rows(1)
-    gate_up(zrecv, hz, 6, 8)
-    loads[2].wait()
-    down_z(0, 0)
-    down_z(0, 1)
-    down_z(0, 2)
-    wait("near", zrecv.at[pl.ds(0, 4)])
-    gate_up(zrecv, hz, 0, 5)
-    down_near()
-    got_rows(2)
-    gate_up(zrecv, hz, 14, 3)
-    down_z(1, 0)
-    down_z(1, 1)
-    down_own(0)
-
-    def down_rest(c):
-        down_z(0, 3)
-        down_z(1, 2)
-        down_z(1, 3)
+    def serve_own():
+        gate_up(xown, hown, 12, 5)
+
+    def serve_near():
+        wait("near", zrecv.at[pl.ds(0, 4)])
+        gate_up(zrecv, hz, 0, 5)
+
+    def serve_early():
+        got_rows(0)
+        got_rows(1)
+        gate_up(zrecv, hz, 6, 8)
+
+    def serve_late():
+        got_rows(2)
+        gate_up(zrecv, hz, 14, 3)
 
     def fill(c, *slots):
         cols = chunk_cols(c)
@@ -464,7 +460,7 @@
 
     def step_five(c):
         wait(f"5{c}", r5p.at[:, double(c)])
-        if c == 0:
+        if not stores:
             wait("sum", zsum)
         for cols in sides(c):
             total = part[0, 0, :, cols].astype(F32) + zsum[:, cols].astype(F32) + r5p[:, cols].astype(F32) + r5m[:, cols].astype(F32)
@@ -474,9 +470,16 @@
         store.start()
         stores.append(store)
 
-    run = {"G": expand, "E": expand_late, "Z": down_rest, "W": down_own, "A": step_two, "B": step_three, "C": step_four, "D": step_five, "F": lambda c: sum_near()}
+    whole = {"O3": serve_own, "N": serve_near, "Z": serve_early, "L": serve_late, "DN": down_near, "F": sum_near}
+    chunked = {
+        "a": functools.partial(down_z, 0), "b": functools.partial(down_z, 1), "W": down_own, "G": expand, "E": expand_late,
+        "A": step_two, "B": step_three, "C": step_four, "D": step_five,
+    }
     for step in STEPS:
-        run[step[0]](int(step[1]))
+        if step in whole:
+            whole[step]()
+        else:
+            chunked[step[0]](int(step[1]))
     assert len(sems) <= MAX_SEMS
     drain("own", gath.at[0])
     drain("pass", gath.at[0])

time: 81.3 us -> 79.1 us (0.973)
  Pallas kernels: 79.5 us -> 77.3 us
    pallas_call x1, Pallas kernels: 79.5 us -> 77.3 us  [shards(): pl.pallas_call(functools.partial(kernel, (n_hi, tok, width, hid, most)),...]
where the time goes in v5:
time: 79.1 us; the launch traced here: 79 us
  Pallas kernels  77.3 us (98%)
  local copies, waits for them, and re-layouts  1.67 us (2%)
    pallas_call x1, Pallas kernels, shards(): pl.pallas_call(functools.partial(kernel, (n_hi, tok, width, hid, most)),...  77.3 us
    unnamed x1, local copies, waits for them, and re-layouts  1.67 us

profile of v5, /device:TPU:1, one launch (start us, length us, event | category | flops | bytes accessed | tf_op | source)
XLA Modules:
  0.0 79.0 jit_solution(9404526276577287437)
XLA Ops:
  0.0 77.3 %routed_experts.1 = bf16[64,2048]{1,0:T(8,128)(2,1)} custom-call(bf16[64,2048]{1,0:T(8,128)(2,1)} %tok_hbm.1, s32[8,64]{1,0:T(8,128)} %bitcast.2, f32[8,64]{1,0:T(8,128)} %bitcast.3, bf16[1,2048,768]{2,1,0:T(8,128)(2,1)} %wg_hbm.1, bf16[1,2048,768]{2,1,0:T(8,128)(2,1)} %wu_hbm.1, bf16[1,768,2048]{2,1,0:T(8,128)(2,1)} %wd_hbm.1), custom_call_target="tpu_custom_call" | custom-call | tf_op jit(solution)/shard_map/routed_experts/pallas_call | solution.py:509
  77.3 1.7 %copy.8 = bf16[64,2048]{1,0:T(8,128)(2,1)} copy(bf16[64,2048]{1,0:T(8,128)(2,1)} %routed_experts.1) | data formatting | bytes 524288

commit v6 on v5

--- a/solution.py
+++ b/solution.py
@@ -18,18 +18,18 @@
 NEAR = {1: "xp", 2: "xm", 3: "yp", 4: "ym"}
 PARTS = (1,) * 8
 STEPS = (
-    "O3", "W2", "Z", "a2", "a3", "N", "L", "DN", "b2", "G4", "b3", "W3", "G5", "W0", "a0", "b0", "W1", "G6", "E4",
-    "E5", "a1", "G7", "E7", "b1", "E6", "G0", "A4", "A5", "E0", "G1", "F", "E1", "B4", "G2", "G3", "E2", "E3", "A7",
-    "A0", "A6", "A2", "A3", "A1", "C4", "B7", "B5", "B6", "B2", "B0", "B3", "B1", "D4", "C5", "C6", "C7", "C2", "C0",
-    "C3", "C1", "D5", "D7", "D3", "D6", "D2", "D0", "D1",
+    "O3", "N", "Z", "a1", "W3", "W1", "L", "b1", "DN", "a2", "b2", "G2", "W2", "E2", "G3", "a3", "E3", "G4", "b3",
+    "G5", "E4", "E5", "A2", "A3", "a0", "G6", "W0", "b0", "G7", "A4", "E7", "E6", "G0", "B2", "G1", "E0", "E1", "A5",
+    "A6", "F", "A7", "A1", "A0", "B5", "B6", "B3", "B7", "B4", "B1", "B0", "C5", "C3", "C6", "C2", "C7", "C1", "C4",
+    "C0", "X", "D7", "D1", "D5", "D4", "D2", "D6", "D3", "D0",
 )
-MAX_SEMS = 128
+LEAVING, LANDING = 22, 75
 
 
 def kernel(
     sizes, tok_hbm, ids_ref, probs_ref, wg_hbm, wu_hbm, wd_hbm, out_hbm,
     gath, meta, comb, xown, zsend, zrecv, hown, hz, wg, wu, wd, zout, both, part, picks,
-    fgath, fmeta, fcomb, fpick, fsend, frecv, fsum, zsum,
+    fgath, fmeta, fcomb, fpick, fsend, frecv, fsum, zsum, esend, erecv,
     r1p, r1m, r2p, r2m, r4p, r4m, r5p, r5m, outv,
     send_sem, recv_sem, local_sem,
 ):
@@ -56,22 +56,26 @@
     }
     other = at(x, y, 1 - z_lo)
 
-    sems = {}
-
-    def sem(array, kind):
-        return array.at[sems.setdefault(kind, len(sems))]
+    leaving, landing = {}, {}
+
+    def sem(array, kinds, kind):
+        return array.at[kinds.setdefault(kind, len(kinds))]
 
     def send(way, src, dst, leaves, lands):
         pltpu.make_async_remote_copy(
-            src_ref=src, dst_ref=dst, send_sem=sem(send_sem, leaves), recv_sem=sem(recv_sem, lands),
+            src_ref=src, dst_ref=dst, send_sem=sem(send_sem, leaving, leaves), recv_sem=sem(recv_sem, landing, lands),
             device_id=target[way], device_id_type=MESH,
         ).start()
 
     def wait(lands, *like):
-        pltpu.make_async_copy(*like, *like, sem(recv_sem, lands)).wait()
+        pltpu.make_async_copy(*like, *like, sem(recv_sem, landing, lands)).wait()
 
     def drain(leaves, like):
-        pltpu.make_async_copy(like, like, sem(send_sem, leaves)).wait()
+        pltpu.make_async_copy(like, like, sem(send_sem, leaving, leaves)).wait()
+
+    barrier = pltpu.get_barrier_semaphore()
+    for way in target:
+        pl.semaphore_signal(barrier, inc=1, device_id=target[way], device_id_type=MESH)
 
     load_tok = pltpu.make_async_copy(tok_hbm, gath.at[0, 0], local_sem.at[0])
     load_tok.start()
@@ -81,10 +85,6 @@
     ]
     for load in loads:
         load.start()
-
-    barrier = pltpu.get_barrier_semaphore()
-    for way in target:
-        pl.semaphore_signal(barrier, inc=1, device_id=target[way], device_id_type=MESH)
 
     ids = ids_ref[...].astype(F32)
     probs = probs_ref[...]
@@ -176,6 +176,11 @@
         comb[place] = scaled.T.astype(BF16)
         picks[place] = one.astype(BF16)
 
+    def ways_out(place):
+        if place == 16:
+            return (("zp", pl.ds(0, most // 2)), ("zm", pl.ds(most // 2, most // 2)))
+        return (("zm" if place % 2 else "zp", pl.ds(0, most)),)
+
     def select(dx, dy):
         place = PLACE[dx, dy]
         rows = most if place < 5 else 2 * most
@@ -190,7 +195,8 @@
 
         if place >= 5:
             group = min((place - 6) // 4, 2)
-            send("zm" if place % 2 else "zp", zsend.at[place], zrecv.at[place], "rows", f"rows{group}")
+            for way, rows in ways_out(place):
+                send(way, zsend.at[place, rows], zrecv.at[place, rows], "rows", f"rows{group}")
 
     def select_all(*slots):
         for slot in slots:
@@ -255,6 +261,39 @@
             gate = jnp.dot(block, wg[:, cols], preferred_element_type=F32)
             up = jnp.dot(block, wu[:, cols], preferred_element_type=F32)
             hidden[place * most:place * most + rows, cols] = (gate / (1.0 + jnp.exp(-gate)) * up).astype(BF16)
+
+    starts = [sum(PARTS[:c]) * width // sum(PARTS) for c in range(len(PARTS) + 1)]
+
+    def chunk_cols(c):
+        return pl.ds(starts[c], starts[c + 1] - starts[c])
+
+    def sides(c):
+        middle = (starts[c] + starts[c + 1]) // 2
+        return pl.ds(starts[c], middle - starts[c]), pl.ds(middle, starts[c + 1] - middle)
+
+    top, low = pl.ds(0, tok // 2), pl.ds(tok // 2, tok // 2)
+
+    def early_own():
+        for q in range(4):
+            out = jnp.dot(hown[0:5 * most, :], wd[:, quarters[q]], preferred_element_type=F32).astype(BF16)
+            for slot, place in PLACE.items():
+                if place < 5:
+                    part[slot[0], slot[1], :, quarters[q]] = jnp.dot(
+                        comb[place, :, :most], out[most * place:most * (place + 1)], preferred_element_type=F32
+                    ).astype(BF16)
+        for c in range(len(PARTS)):
+            left, right = sides(c)
+            esend[0, :, early_cols(c)] = part[0, 1, low, left]
+            esend[1, :, early_cols(c)] = part[0, 3, top, left]
+            esend[2, :, early_cols(c)] = part[1, 0, low, right]
+            esend[3, :, early_cols(c)] = part[3, 0, top, right]
+
+    def early_cols(c):
+        return pl.ds(starts[c] // 2, (starts[c + 1] - starts[c]) // 2)
+
+    def send_early():
+        for i, way in enumerate(("yp", "ym", "xp", "xm")):
+            send(way, esend.at[i], erecv.at[i], "early", "early")
 
     own_first()
     own_second()
@@ -282,6 +321,7 @@
     got_far()
     passes(2)
     gate_up(xown, hown, 0, 5, 2, 3)
+    early_own()
     got_passes(3)
     relays(1)
     relays(3)
@@ -292,6 +332,7 @@
     got_passes(2)
     relays(2)
     send_near()
+    send_early()
     gate_up(xown, hown, 6, 6, 1, 3)
     got_relays(1)
     select_all((1, 2), (2, 1))
@@ -300,17 +341,6 @@
     got_relays(2)
     select_all((2, 2))
 
-    starts = [sum(PARTS[:c]) * width // sum(PARTS) for c in range(len(PARTS) + 1)]
-
-    def chunk_cols(c):
-        return pl.ds(starts[c], starts[c + 1] - starts[c])
-
-    def sides(c):
-        middle = (starts[c] + starts[c + 1]) // 2
-        return pl.ds(starts[c], middle - starts[c]), pl.ds(middle, starts[c + 1] - middle)
-
-    top, low = pl.ds(0, tok // 2), pl.ds(tok // 2, tok // 2)
-
     def quarter_chunks(q):
         return [c for c in range(len(PARTS)) if q * quarter <= starts[c] < (q + 1) * quarter]
 
@@ -321,14 +351,17 @@
         for i in range(places):
             zout[(place + i) // 2, (place + i) % 2, :, quarters[q]] = out[most * i:most * (i + 1)]
         for c in quarter_chunks(q):
-            for side, way in ((0, "zm"), (1, "zp")):
-                pairs = pl.ds(place // 2, (places + 1 - side) // 2)
-                send(
-                    way,
-                    zout.at[pairs, side, :, chunk_cols(c)],
-                    both.at[pairs, side, pl.ds(most, most), chunk_cols(c)],
-                    "back", f"back{part_of}{c}",
-                )
+            cols, kind = chunk_cols(c), f"back{part_of}{c}"
+            if part_of == 0:
+                for side, way in ((0, "zm"), (1, "zp")):
+                    pairs = pl.ds(place // 2, places // 2)
+                    send(way, zout.at[pairs, side, :, cols], both.at[pairs, side, pl.ds(most, most), cols], "back", kind)
+            else:
+                for i in range(places):
+                    pair, side = (place + i) // 2, (place + i) % 2
+                    for way, rows in ways_out(place + i):
+                        to = pl.ds(most + rows.start, rows.size)
+                        send(OPPOSITE[way], zout.at[pair, side, rows, cols], both.at[pair, side, to, cols], "back", kind)
 
     def down_near():
         @pl.loop(0, 4, unroll=4)
@@ -341,9 +374,10 @@
         back_near()
 
     def down_own(q):
-        out = jnp.dot(hown[...], wd[:, quarters[q]], preferred_element_type=F32).astype(BF16)
-        for place in PLACE.values():
-            both[place // 2, place % 2, 0:most, quarters[q]] = out[most * place:most * (place + 1)]
+        rows = hown[6 * most:17 * most, :]
+        out = jnp.dot(rows, wd[:, quarters[q]], preferred_element_type=F32).astype(BF16)
+        for place in range(6, 17):
+            both[place // 2, place % 2, 0:most, quarters[q]] = out[most * (place - 6):most * (place - 5)]
 
     def serve_own():
         gate_up(xown, hown, 12, 5)
@@ -365,9 +399,8 @@
         cols = chunk_cols(c)
         for dx, dy in slots:
             place = PLACE[dx, dy]
-            rows = most if place < 5 else 2 * most
             part[dx, dy, :, cols] = jnp.dot(
-                comb[place, :, :rows], both[place // 2, place % 2, :rows, cols], preferred_element_type=F32
+                comb[place], both[place // 2, place % 2, :, cols], preferred_element_type=F32
             ).astype(BF16)
 
     late = ((3, 2), (2, 3), (2, 2))
@@ -384,11 +417,11 @@
         wait(f"back0{c}", zrecv.at[pl.ds(0, 8), :, chunk_cols(c)])
         fill(c, (0, 2), (1, 2), (2, 0), (2, 1))
         halves_one(c, pl.ds(0, 2))
-        fill(c, *[slot for slot in PLACE if 2 not in slot])
-        send("yp", part.at[:, 1, low, left], r2p.at[:, low, left], "2p", f"2{c}")
-        send("xp", part.at[1, :, low, right], r2p.at[:, low, right], "2p", f"2{c}")
-        send("ym", part.at[pl.ds(0, 2), 3, top, left], r2m.at[pl.ds(0, 2), top, left], "2m", f"2{c}")
-        send("xm", part.at[3, pl.ds(0, 2), top, right], r2m.at[pl.ds(0, 2), top, right], "2m", f"2{c}")
+        fill(c, (1, 1), (3, 3), (1, 3), (3, 1))
+        send("yp", part.at[pl.ds(1, 3), 1, low, left], r2p.at[pl.ds(1, 3), low, left], "2p", f"2{c}")
+        send("xp", part.at[1, pl.ds(1, 3), low, right], r2p.at[pl.ds(1, 3), low, right], "2p", f"2{c}")
+        send("ym", part.at[1, 3, top, left], r2m.at[1, top, left], "2m", f"2{c}")
+        send("xm", part.at[3, 1, top, right], r2m.at[1, top, right], "2m", f"2{c}")
 
     def expand_late(c):
         left, right = sides(c)
@@ -433,10 +466,20 @@
             add(3, d, low, right, r1m.at[d, :, right])
         halves_two(c, top, low)
 
+    got = []
+
     def step_three(c):
         left, right = sides(c)
-        wait(f"2{c}", r2p.at[:, :, double(c)])
+        wait(f"2{c}", both.at[pl.ds(0, 7), 0, :, chunk_cols(c)])
+        if "early" not in got:
+            got.append("early")
+            wait("early", erecv)
         for d in (2, 1, 3, 0):
+            if d == 0:
+                for cols, plus, minus in ((left, 0, 1), (right, 2, 3)):
+                    add(0, 0, top, cols, r2p.at[0, top, cols], erecv.at[minus, :, early_cols(c)])
+                    add(0, 0, low, cols, erecv.at[plus, :, early_cols(c)], r2m.at[0, low, cols])
+                continue
             add(d, 0, every, left, r2p.at[d, :, left], r2m.at[d, :, left])
             add(0, d, every, right, r2p.at[d, :, right], r2m.at[d, :, right])
             if d == 2:
@@ -458,6 +501,7 @@
 
     stores = []
 
+
     def step_five(c):
         wait(f"5{c}", r5p.at[:, double(c)])
         if not stores:
@@ -466,11 +510,31 @@
             total = part[0, 0, :, cols].astype(F32) + zsum[:, cols].astype(F32) + r5p[:, cols].astype(F32) + r5m[:, cols].astype(F32)
             outv[:, cols] = total.astype(BF16)
         cols = chunk_cols(c)
-        store = pltpu.make_async_copy(outv.at[:, cols], out_hbm.at[:, cols], local_sem.at[4 + c])
+        store = pltpu.make_async_copy(outv.at[:, cols], out_hbm.at[:, cols], local_sem.at[4])
         store.start()
-        stores.append(store)
-
-    whole = {"O3": serve_own, "N": serve_near, "Z": serve_early, "L": serve_late, "DN": down_near, "F": sum_near}
+        stores.append(c)
+
+    def drain_all(c=0):
+        drain("own", gath.at[0])
+        drain("pass", gath.at[0])
+        drain("second", gath.at[0, 0:3])
+        drain("relay", gath.at[0])
+        drain("m12", meta.at[0:3])
+        drain("m3", meta.at[0, 0:3])
+        for kind in ("rows", "back"):
+            drain(kind, zsend.at[pl.ds(0, 11)])
+        for kind in ("near", "nearback"):
+            drain(kind, frecv)
+        drain("whole", fgath)
+        drain("mwhole", fmeta)
+        drain("sum", fsum)
+        drain("early", esend)
+        for kind, like in (("1p", r1p), ("1m", r1m), ("4p", r4p), ("4m", r4m)):
+            drain(kind, like)
+        for kind in ("2p", "2m"):
+            drain(kind, both.at[pl.ds(0, 7), 0, :, first])
+
+    whole = {"O3": serve_own, "N": serve_near, "Z": serve_early, "L": serve_late, "DN": down_near, "F": sum_near, "X": drain_all}
     chunked = {
         "a": functools.partial(down_z, 0), "b": functools.partial(down_z, 1), "W": down_own, "G": expand, "E": expand_late,
         "A": step_two, "B": step_three, "C": step_four, "D": step_five,
@@ -480,24 +544,10 @@
             whole[step]()
         else:
             chunked[step[0]](int(step[1]))
-    assert len(sems) <= MAX_SEMS
-    drain("own", gath.at[0])
-    drain("pass", gath.at[0])
-    drain("second", gath.at[0, 0:3])
-    drain("relay", gath.at[0])
-    drain("m12", meta.at[0:3])
-    drain("m3", meta.at[0, 0:3])
-    drain("rows", zsend.at[pl.ds(0, 11)])
-    drain("back", zsend.at[pl.ds(0, 11)])
-    drain("near", frecv)
-    drain("nearback", frecv)
-    drain("whole", fgath)
-    drain("mwhole", fmeta)
-    drain("sum", fsum)
-    for kind, like in (("1p", r1p), ("1m", r1m), ("2p", r2p), ("2m", r2m), ("4p", r4p), ("4m", r4m), ("5p", r5p), ("5m", r5m)):
-        drain(kind, like)
-    for store in stores:
-        store.wait()
+    assert (len(leaving), len(landing)) == (LEAVING, LANDING), (len(leaving), len(landing))
+    drain("5p", r5p)
+    drain("5m", r5m)
+    pltpu.make_async_copy(outv, out_hbm, local_sem.at[4]).wait()
 
 
 def shards(n_hi, tokens, expert_ids, gate_probs, w_gate, w_up, w_down):
@@ -535,6 +585,8 @@
             pltpu.VMEM((4, most, width), BF16),
             pltpu.VMEM((tok, width), BF16),
             pltpu.VMEM((tok, width), BF16),
+            pltpu.VMEM((4, tok // 2, width // 2), BF16),
+            pltpu.VMEM((4, tok // 2, width // 2), BF16),
             pltpu.VMEM((4, tok // 2, width), BF16),
             pltpu.VMEM((4, tok // 2, width), BF16),
             pltpu.VMEM((4, tok, width), BF16),
@@ -544,9 +596,9 @@
             pltpu.VMEM((tok, width), BF16),
             pltpu.VMEM((tok, width), BF16),
             pltpu.VMEM((tok, width), BF16),
-            pltpu.SemaphoreType.DMA((MAX_SEMS,)),
-            pltpu.SemaphoreType.DMA((MAX_SEMS,)),
-            pltpu.SemaphoreType.DMA((4 + len(PARTS),)),
+            pltpu.SemaphoreType.DMA((LEAVING,)),
+            pltpu.SemaphoreType.DMA((LANDING,)),
+            pltpu.SemaphoreType.DMA((5,)),
         ],
         compiler_params=pltpu.CompilerParams(
             collective_id=0, has_side_effects=True, vmem_limit_bytes=60 * 1024 * 1024

time: 79.1 us -> 76.1 us (0.962)
  Pallas kernels: 77.3 us -> 74.2 us
    pallas_call x1, Pallas kernels: 77.3 us -> 74.2 us  [shards(): pl.pallas_call(functools.partial(kernel, (n_hi, tok, width, hid, most)),...]
where the time goes in v6:
time: 76.1 us; the launch traced here: 75.9 us
  Pallas kernels  74.2 us (98%)
  local copies, waits for them, and re-layouts  1.67 us (2%)
    pallas_call x1, Pallas kernels, shards(): pl.pallas_call(functools.partial(kernel, (n_hi, tok, width, hid, most)),...  74.2 us
    unnamed x1, local copies, waits for them, and re-layouts  1.67 us

profile of v6, /device:TPU:1, one launch (start us, length us, event | category | flops | bytes accessed | tf_op | source)
XLA Modules:
  0.0 75.9 jit_solution(15220501286728522064)
XLA Ops:
  0.0 74.2 %routed_experts.1 = bf16[64,2048]{1,0:T(8,128)(2,1)} custom-call(bf16[64,2048]{1,0:T(8,128)(2,1)} %tok_hbm.1, s32[8,64]{1,0:T(8,128)} %bitcast.2, f32[8,64]{1,0:T(8,128)} %bitcast.3, bf16[1,2048,768]{2,1,0:T(8,128)(2,1)} %wg_hbm.1, bf16[1,2048,768]{2,1,0:T(8,128)(2,1)} %wu_hbm.1, bf16[1,768,2048]{2,1,0:T(8,128)(2,1)} %wd_hbm.1), custom_call_target="tpu_custom_call" | custom-call | tf_op jit(solution)/shard_map/routed_experts/pallas_call | solution.py:559
  74.3 1.7 %copy.8 = bf16[64,2048]{1,0:T(8,128)(2,1)} copy(bf16[64,2048]{1,0:T(8,128)(2,1)} %routed_experts.1) | data formatting | bytes 524288

commit v7 on v6

--- a/solution.py
+++ b/solution.py
@@ -18,12 +18,12 @@
 NEAR = {1: "xp", 2: "xm", 3: "yp", 4: "ym"}
 PARTS = (1,) * 8
 STEPS = (
-    "O3", "N", "Z", "a1", "W3", "W1", "L", "b1", "DN", "a2", "b2", "G2", "W2", "E2", "G3", "a3", "E3", "G4", "b3",
-    "G5", "E4", "E5", "A2", "A3", "a0", "G6", "W0", "b0", "G7", "A4", "E7", "E6", "G0", "B2", "G1", "E0", "E1", "A5",
-    "A6", "F", "A7", "A1", "A0", "B5", "B6", "B3", "B7", "B4", "B1", "B0", "C5", "C3", "C6", "C2", "C7", "C1", "C4",
-    "C0", "X", "D7", "D1", "D5", "D4", "D2", "D6", "D3", "D0",
+    "O3", "Z", "a3", "W3", "a1", "N", "DN", "L", "W2", "G6", "W1", "b1", "b3", "a0", "G7", "W0", "G2", "G3", "E2",
+    "b0", "E3", "E6", "b2", "a2", "E7", "G0", "A2", "A3", "G1", "E0", "A7", "A6", "E1", "G4", "E4", "F", "G5", "E5",
+    "A1", "A0", "A4", "B7", "A5", "B2", "B1", "B6", "B0", "B3", "B4", "B5", "C7", "C1", "C0", "C2", "C6", "C4", "C3",
+    "C5", "X", "D4", "D0", "D3", "D1", "D6", "D7", "D2", "D5",
 )
-LEAVING, LANDING = 22, 75
+LEAVING, LANDING = 21, 73
 
 
 def kernel(
@@ -97,8 +97,8 @@
     ranks = jnp.dot(named.astype(BF16), before.astype(F32).astype(BF16), preferred_element_type=F32)
     for k in range(8):
         rank = jnp.sum(jnp.where(ids[k:k + 1, :] == experts, ranks, 0.0), axis=0, keepdims=True)
-        meta[0, 0, k:k + 1, 0:tok] = ids[k:k + 1, :] * float(most) + rank
-    meta[0, 0, 8:16, 0:tok] = weights
+        meta[0, k:k + 1, 0:tok] = ids[k:k + 1, :] * float(most) + rank
+    meta[0, :, tok:2 * tok] = weights
 
     pl.semaphore_wait(barrier, 6)
     load_tok.wait()
@@ -106,19 +106,19 @@
     first, second = pl.ds(0, half), pl.ds(half, half)
     quarters = [pl.ds(q * quarter, quarter) for q in range(4)]
 
-    def move(kind, leaves, way, slot, cols, with_meta=None):
+    def move(kind, leaves, way, slot, cols, with_meta=False):
         dx, dy = slot
         shift = {"xp": (3, 0), "xm": (1, 0), "yp": (0, 3), "ym": (0, 1)}[way]
         to = ((dx + shift[0]) % 4, (dy + shift[1]) % 4)
         send(way, gath.at[dx, dy, :, cols], gath.at[to[0], to[1], :, cols], leaves, kind)
         if with_meta:
-            send(way, meta.at[dx, dy], meta.at[to[0], to[1]], with_meta, "m" + kind)
+            send(way, meta.at[4 * dx + dy], meta.at[4 * to[0] + to[1]], "meta", "m" + kind)
 
     def own_first():
         for way in ("xp", "xm"):
-            move("own", "own", way, (0, 0), first, "m12")
+            move("own", "own", way, (0, 0), first, True)
         for way in ("yp", "ym"):
-            move("own", "own", way, (0, 0), second, "m3")
+            move("own", "own", way, (0, 0), second, True)
 
     def own_second():
         for way in ("yp", "ym"):
@@ -127,41 +127,41 @@
             move("pass0", "own", way, (0, 0), second)
 
     def own_relay():
-        move("far", "pass", "xp", (3, 0), quarters[0], "m12")
+        move("far", "pass", "xp", (3, 0), quarters[0], True)
         move("far", "pass", "xm", (1, 0), quarters[1])
-        move("far", "pass", "yp", (0, 3), quarters[2], "m3")
+        move("far", "pass", "yp", (0, 3), quarters[2], True)
         move("far", "pass", "ym", (0, 1), quarters[3])
 
     def passes(d):
         e = (4 - d) % 4
-        move(f"pass{d}", "pass", "ym", (d, 0), first, "m12")
-        move(f"pass{d}", "second", "xm", (0, d), second)
-        move(f"pass{d}", "pass", "yp", (e, 0), first, "m12")
-        move(f"pass{d}", "second", "xp", (0, e), second)
+        move(f"pass{d}", "pass", "ym", (d, 0), first, d > 1)
+        move(f"pass{d}", "second", "xm", (0, d), second, d < 3)
+        move(f"pass{d}", "pass", "yp", (e, 0), first, d > 1)
+        move(f"pass{d}", "second", "xp", (0, e), second, d < 3)
 
     def relays(d):
-        move(f"relay{d}", "relay", "yp", (d, 3), quarters[0], "m12" if d else None)
-        move(f"relay{d}", "relay", "ym", (d, 1), quarters[1])
+        move(f"relay{d}", "relay", "yp", (d, 3), quarters[0])
+        move(f"relay{d}", "relay", "ym", (d, 1), quarters[1], d == 2)
         move(f"relay{d}", "relay", "xp", (3, d), quarters[2])
         move(f"relay{d}", "relay", "xm", (1, d), quarters[3])
 
     def got_own():
         wait("own", gath.at[0, 0:2])
-        wait("mown", meta.at[0])
+        wait("mown", meta.at[pl.ds(0, 4)])
 
     def got_far():
         wait("far", gath.at[0, 0])
-        wait("mfar", meta.at[0, 0:2])
+        wait("mfar", meta.at[pl.ds(0, 2)])
 
     def got_passes(d):
         wait(f"pass{d}", gath.at[0, 0:2])
         if d:
-            wait(f"mpass{d}", meta.at[0, 0:2])
+            wait(f"mpass{d}", meta.at[pl.ds(0, 4 if d == 2 else 2)])
 
     def got_relays(d):
         wait(f"relay{d}", gath.at[0, 0])
-        if d:
-            wait(f"mrelay{d}", meta.at[0, 0])
+        if d == 2:
+            wait("mrelay2", meta.at[0])
 
     place_row = lax.broadcasted_iota(jnp.int32, (2 * most, tok), 0)
     wanted = jnp.where(place_row < most, ep * most + place_row, (other - 1) * most + place_row).astype(F32)
@@ -169,10 +169,12 @@
     def build(dx, dy):
         place = PLACE[dx, dy]
         one, scaled = jnp.zeros((2 * most, tok), F32), jnp.zeros((2 * most, tok), F32)
+        routes = meta[4 * dx + dy]
+        codes, shares_of = routes[:, 0:tok], routes[:, tok:2 * tok]
         for k in range(8):
-            hit = meta[dx, dy, k:k + 1, 0:tok] == wanted
+            hit = codes[k:k + 1, :] == wanted
             one = one + jnp.where(hit, 1.0, 0.0)
-            scaled = scaled + jnp.where(hit, meta[dx, dy, 8 + k:9 + k, 0:tok], 0.0)
+            scaled = scaled + jnp.where(hit, shares_of[k:k + 1, :], 0.0)
         comb[place] = scaled.T.astype(BF16)
         picks[place] = one.astype(BF16)
 
@@ -209,13 +211,15 @@
     near_experts = (ep, at(lax.rem(x + 1, 4), y, z_lo), at(lax.rem(x + 3, 4), y, z_lo), at(x, lax.rem(y + 1, 4), z_lo), at(x, lax.rem(y + 3, 4), z_lo))
 
     def select_foreign():
+        routes = fmeta[...]
+        codes, shares_of = routes[:, 0:tok], routes[:, tok:2 * tok]
         for i, expert in enumerate(near_experts):
             row = (expert * most + lax.broadcasted_iota(jnp.int32, (most, tok), 0)).astype(F32)
             one, scaled = jnp.zeros((most, tok), F32), jnp.zeros((most, tok), F32)
             for k in range(8):
-                hit = fmeta[k:k + 1, 0:tok] == row
+                hit = codes[k:k + 1, :] == row
                 one = one + jnp.where(hit, 1.0, 0.0)
-                scaled = scaled + jnp.where(hit, fmeta[8 + k:9 + k, 0:tok], 0.0)
+                scaled = scaled + jnp.where(hit, shares_of[k:k + 1, :], 0.0)
             fcomb[i] = scaled.T.astype(BF16)
             fpick[i * most:(i + 1) * most, :] = one.astype(BF16)
 
@@ -298,7 +302,7 @@
     own_first()
     own_second()
     send("zm", gath.at[0, 0], fgath, "whole", "whole")
-    send("zm", meta.at[0, 0], fmeta, "mwhole", "mwhole")
+    send("zm", meta.at[0], fmeta, "mwhole", "mwhole")
     select_all((0, 0))
     got_own()
     passes(1)
@@ -338,6 +342,8 @@
     select_all((1, 2), (2, 1))
     got_relays(3)
     select_all((3, 2), (2, 3))
+    got_rows(0)
+    gate_up(zrecv, hz, 6, 4)
     got_relays(2)
     select_all((2, 2))
 
@@ -387,9 +393,8 @@
         gate_up(zrecv, hz, 0, 5)
 
     def serve_early():
-        got_rows(0)
         got_rows(1)
-        gate_up(zrecv, hz, 6, 8)
+        gate_up(zrecv, hz, 10, 4)
 
     def serve_late():
         got_rows(2)
@@ -519,8 +524,7 @@
         drain("pass", gath.at[0])
         drain("second", gath.at[0, 0:3])
         drain("relay", gath.at[0])
-        drain("m12", meta.at[0:3])
-        drain("m3", meta.at[0, 0:3])
+        drain("meta", meta.at[pl.ds(0, 15)])
         for kind in ("rows", "back"):
             drain(kind, zsend.at[pl.ds(0, 11)])
         for kind in ("near", "nearback"):
@@ -563,7 +567,7 @@
         out_specs=hbm,
         scratch_shapes=[
             pltpu.VMEM((4, 4, tok, width), BF16),
-            pltpu.VMEM((4, 4, 16, 128), F32),
+            pltpu.VMEM((16, 8, 128), F32),
             pltpu.VMEM((PLACES, tok, 2 * most), BF16),
             pltpu.VMEM((PLACES, most, width), BF16),
             pltpu.VMEM((PLACES, most, width), BF16),
@@ -578,7 +582,7 @@
             pltpu.VMEM((4, 4, tok, width), BF16),
             pltpu.VMEM((PLACES, 2 * most, tok), BF16),
             pltpu.VMEM((tok, width), BF16),
-            pltpu.VMEM((16, 128), F32),
+            pltpu.VMEM((8, 128), F32),
             pltpu.VMEM((5, tok, most), BF16),
             pltpu.VMEM((5 * most, tok), BF16),
             pltpu.VMEM((4, most, width), BF16),

time: 76.1 us -> 73.6 us (0.967)
  Pallas kernels: 74.2 us -> 71.8 us
    pallas_call x1, Pallas kernels: 74.2 us -> 71.8 us  [shards(): pl.pallas_call(functools.partial(kernel, (n_hi, tok, width, hid, most)),...]
where the time goes in v7:
time: 73.6 us; the launch traced here: 73.5 us
  Pallas kernels  71.8 us (98%)
  local copies, waits for them, and re-layouts  1.67 us (2%)
    pallas_call x1, Pallas kernels, shards(): pl.pallas_call(functools.partial(kernel, (n_hi, tok, width, hid, most)),...  71.8 us
    unnamed x1, local copies, waits for them, and re-layouts  1.67 us

profile of v7, /device:TPU:1, one launch (start us, length us, event | category | flops | bytes accessed | tf_op | source)
XLA Modules:
  0.0 73.5 jit_solution(13014536941971592068)
XLA Ops:
  0.0 71.8 %routed_experts.1 = bf16[64,2048]{1,0:T(8,128)(2,1)} custom-call(bf16[64,2048]{1,0:T(8,128)(2,1)} %tok_hbm.1, s32[8,64]{1,0:T(8,128)} %bitcast.2, f32[8,64]{1,0:T(8,128)} %bitcast.3, bf16[1,2048,768]{2,1,0:T(8,128)(2,1)} %wg_hbm.1, bf16[1,2048,768]{2,1,0:T(8,128)(2,1)} %wu_hbm.1, bf16[1,768,2048]{2,1,0:T(8,128)(2,1)} %wd_hbm.1), custom_call_target="tpu_custom_call" | custom-call | tf_op jit(solution)/shard_map/routed_experts/pallas_call | solution.py:563
  71.8 1.7 %copy.8 = bf16[64,2048]{1,0:T(8,128)(2,1)} copy(bf16[64,2048]{1,0:T(8,128)(2,1)} %routed_experts.1) | data formatting | bytes 524288

commit v8 on v7

--- a/solution.py
+++ b/solution.py
@@ -27,7 +27,7 @@
 
 
 def kernel(
-    sizes, tok_hbm, ids_ref, probs_ref, wg_hbm, wu_hbm, wd_hbm, out_hbm,
+    sizes, tok_hbm, routes_ref, wg_hbm, wu_hbm, wd_hbm, out_hbm,
     gath, meta, comb, xown, zsend, zrecv, hown, hz, wg, wu, wd, zout, both, part, picks,
     fgath, fmeta, fcomb, fpick, fsend, frecv, fsum, zsum, esend, erecv,
     r1p, r1m, r2p, r2m, r4p, r4m, r5p, r5m, outv,
@@ -86,8 +86,8 @@
     for load in loads:
         load.start()
 
-    ids = ids_ref[...].astype(F32)
-    probs = probs_ref[...]
+    ids = jnp.floor(routes_ref[...] * 0.5)
+    probs = routes_ref[...] - 2.0 * ids
     weights = probs / jnp.sum(probs, axis=0, keepdims=True)
     experts = lax.broadcasted_iota(jnp.int32, (32, tok), 0).astype(F32)
     named = jnp.zeros((32, tok), F32)
@@ -560,10 +560,11 @@
     most = 32
     vmem = pl.BlockSpec(memory_space=pltpu.VMEM)
     hbm = pl.BlockSpec(memory_space=pl.ANY)
+    routes = (expert_ids.astype(F32) * 2.0 + gate_probs).T
     return pl.pallas_call(
         functools.partial(kernel, (n_hi, tok, width, hid, most)),
         out_shape=jax.ShapeDtypeStruct((tok, width), BF16),
-        in_specs=[hbm, vmem, vmem, hbm, hbm, hbm],
+        in_specs=[hbm, vmem, hbm, hbm, hbm],
         out_specs=hbm,
         scratch_shapes=[
             pltpu.VMEM((4, 4, tok, width), BF16),
@@ -605,10 +606,10 @@
             pltpu.SemaphoreType.DMA((5,)),
         ],
         compiler_params=pltpu.CompilerParams(
-            collective_id=0, has_side_effects=True, vmem_limit_bytes=60 * 1024 * 1024
+            collective_id=0, has_side_effects=True, vmem_limit_bytes=54784 * 1024
         ),
         name="routed_experts",
-    )(tokens, expert_ids.T, gate_probs.T, w_gate, w_up, w_down)
+    )(tokens, routes, w_gate, w_up, w_down)
 
 
 def solution(mesh):

time: 73.6 us -> 72 us (0.978)
  Pallas kernels: 71.8 us -> 70.5 us
  local copies, waits for them, and re-layouts: 1.67 us -> 0.71 us
    pallas_call x1, Pallas kernels: 71.8 us -> 70.5 us  [shards(): pl.pallas_call(functools.partial(kernel, (n_hi, tok, width, hid, most)),...]
    unnamed x1, local copies, waits for them, and re-layouts: 1.67 us -> 0.71 us
where the time goes in v8:
time: 72 us; the launch traced here: 71.9 us
  Pallas kernels  70.5 us (98%)
    pallas_call x1, Pallas kernels, shards(): pl.pallas_call(functools.partial(kernel, (n_hi, tok, width, hid, most)),...  70.5 us

profile of v8, /device:TPU:1, one launch (start us, length us, event | category | flops | bytes accessed | tf_op | source)
XLA Modules:
  0.0 71.9 jit_solution(5311959799980529624)
XLA Ops:
  0.0 0.7 add_bitcast_fusion.routes_ref
  0.7 70.5 %routed_experts.1 = bf16[64,2048]{1,0:T(8,128)(2,1)S(1)} custom-call(bf16[64,2048]{1,0:T(8,128)(2,1)} %tok_hbm.1, f32[8,64]{1,0:T(8,128)S(1)} %add_bitcast_fusion.routes_ref, bf16[1,2048,768]{2,1,0:T(8,128)(2,1)} %wg_hbm.1, bf16[1,2048,768]{2,1,0:T(8,128)(2,1)} %wu_hbm.1, bf16[1,768,2048]{2,1,0:T(8,128)(2,1)} %wd_hbm.1), custom_call_target="tpu_custom_call" | custom-call | tf_op jit(solution)/shard_map/routed_experts/pallas_call | solution.py:564
  71.2 0.7 copy.8

commit v9 on v8

--- a/solution.py
+++ b/solution.py
@@ -23,14 +23,14 @@
     "A1", "A0", "A4", "B7", "A5", "B2", "B1", "B6", "B0", "B3", "B4", "B5", "C7", "C1", "C0", "C2", "C6", "C4", "C3",
     "C5", "X", "D4", "D0", "D3", "D1", "D6", "D7", "D2", "D5",
 )
-LEAVING, LANDING = 21, 73
+LEAVING, LANDING = 21, 57
 
 
 def kernel(
-    sizes, tok_hbm, routes_ref, wg_hbm, wu_hbm, wd_hbm, out_hbm,
+    sizes, tok_hbm, routes_ref, wg_hbm, wu_hbm, wd_hbm, out_ref,
     gath, meta, comb, xown, zsend, zrecv, hown, hz, wg, wu, wd, zout, both, part, picks,
     fgath, fmeta, fcomb, fpick, fsend, frecv, fsum, zsum, esend, erecv,
-    r1p, r1m, r2p, r2m, r4p, r4m, r5p, r5m, outv,
+    r1p, r1m, r2p, r2m, r4p, r4m, r5p, r5m,
     send_sem, recv_sem, local_sem,
 ):
     n_hi, tok, width, hid, most = sizes
@@ -238,10 +238,10 @@
     def back_near():
         for place, way in NEAR.items():
             index = ("xm", "xp", "ym", "yp").index(way)
-            send(way, zout.at[place // 2, place % 2], frecv.at[index], "nearback", "nearback")
+            send(way, zout.at[place // 2, place % 2], frecv.at[index], "nb", "nb")
 
     def sum_near():
-        wait("nearback", frecv)
+        wait("nb", frecv)
 
         @pl.loop(0, 4, unroll=4)
         def _(q):
@@ -302,7 +302,7 @@
     own_first()
     own_second()
     send("zm", gath.at[0, 0], fgath, "whole", "whole")
-    send("zm", meta.at[0], fmeta, "mwhole", "mwhole")
+    send("zm", meta.at[0], fmeta, "mw", "mw")
     select_all((0, 0))
     got_own()
     passes(1)
@@ -315,7 +315,7 @@
     for slot in CLUSTER[1:]:
         select(*slot)
     wait("whole", fgath)
-    wait("mwhole", fmeta)
+    wait("mw", fmeta)
     select_foreign()
     for load in loads:
         load.wait()
@@ -342,10 +342,10 @@
     select_all((1, 2), (2, 1))
     got_relays(3)
     select_all((3, 2), (2, 3))
+    got_relays(2)
+    select_all((2, 2))
     got_rows(0)
     gate_up(zrecv, hz, 6, 4)
-    got_relays(2)
-    select_all((2, 2))
 
     def quarter_chunks(q):
         return [c for c in range(len(PARTS)) if q * quarter <= starts[c] < (q + 1) * quarter]
@@ -357,7 +357,7 @@
         for i in range(places):
             zout[(place + i) // 2, (place + i) % 2, :, quarters[q]] = out[most * i:most * (i + 1)]
         for c in quarter_chunks(q):
-            cols, kind = chunk_cols(c), f"back{part_of}{c}"
+            cols, kind = chunk_cols(c), "uv"[part_of] + str(c)
             if part_of == 0:
                 for side, way in ((0, "zm"), (1, "zp")):
                     pairs = pl.ds(place // 2, places // 2)
@@ -419,7 +419,7 @@
 
     def expand(c):
         left, right = sides(c)
-        wait(f"back0{c}", zrecv.at[pl.ds(0, 8), :, chunk_cols(c)])
+        wait(f"u{c}", zrecv.at[pl.ds(0, 8), :, chunk_cols(c)])
         fill(c, (0, 2), (1, 2), (2, 0), (2, 1))
         halves_one(c, pl.ds(0, 2))
         fill(c, (1, 1), (3, 3), (1, 3), (3, 1))
@@ -430,7 +430,7 @@
 
     def expand_late(c):
         left, right = sides(c)
-        wait(f"back1{c}", zrecv.at[pl.ds(0, 3), :, chunk_cols(c)])
+        wait(f"v{c}", zrecv.at[pl.ds(0, 3), :, chunk_cols(c)])
         fill(c, *late)
         halves_one(c, pl.ds(2, 2))
         send("ym", part.at[pl.ds(2, 2), 3, top, left], r2m.at[pl.ds(2, 2), top, left], "2m", f"2{c}")
@@ -445,10 +445,10 @@
 
     def halves_five(c, plus, minus):
         left, right = sides(c)
-        send("xp", part.at[1, 0, plus, left], r5p.at[plus, left], "5p", f"5{c}")
-        send("xm", part.at[3, 0, minus, left], r5m.at[minus, left], "5m", f"5{c}")
-        send("yp", part.at[0, 1, plus, right], r5p.at[plus, right], "5p", f"5{c}")
-        send("ym", part.at[0, 3, minus, right], r5m.at[minus, right], "5m", f"5{c}")
+        send("xp", part.at[1, 0, plus, left], r5p.at[plus, left], "5p", f"v{c}")
+        send("xm", part.at[3, 0, minus, left], r5m.at[minus, left], "5m", f"v{c}")
+        send("yp", part.at[0, 1, plus, right], r5p.at[plus, right], "5p", f"v{c}")
+        send("ym", part.at[0, 3, minus, right], r5m.at[minus, right], "5m", f"v{c}")
 
     def double(c):
         return pl.ds(0, 2 * chunk_cols(c).size)
@@ -488,16 +488,16 @@
             add(d, 0, every, left, r2p.at[d, :, left], r2m.at[d, :, left])
             add(0, d, every, right, r2p.at[d, :, right], r2m.at[d, :, right])
             if d == 2:
-                send("xp", part.at[2, 0, top, left], r4p.at[:, left], "4p", f"4{c}")
-                send("xm", part.at[2, 0, low, left], r4m.at[:, left], "4m", f"4{c}")
-                send("yp", part.at[0, 2, top, right], r4p.at[:, right], "4p", f"4{c}")
-                send("ym", part.at[0, 2, low, right], r4m.at[:, right], "4m", f"4{c}")
+                send("xp", part.at[2, 0, top, left], r4p.at[:, left], "4p", f"u{c}")
+                send("xm", part.at[2, 0, low, left], r4m.at[:, left], "4m", f"u{c}")
+                send("yp", part.at[0, 2, top, right], r4p.at[:, right], "4p", f"u{c}")
+                send("ym", part.at[0, 2, low, right], r4m.at[:, right], "4m", f"u{c}")
             if d == 3:
                 halves_five(c, low, top)
 
     def step_four(c):
         left, right = sides(c)
-        wait(f"4{c}", r4p.at[:, double(c)])
+        wait(f"u{c}", r4p.at[:, double(c)])
         add(1, 0, top, left, r4p.at[:, left])
         add(3, 0, low, left, r4m.at[:, left])
         add(0, 1, top, right, r4p.at[:, right])
@@ -508,15 +508,12 @@
 
 
     def step_five(c):
-        wait(f"5{c}", r5p.at[:, double(c)])
+        wait(f"v{c}", r5p.at[:, double(c)])
         if not stores:
             wait("sum", zsum)
         for cols in sides(c):
             total = part[0, 0, :, cols].astype(F32) + zsum[:, cols].astype(F32) + r5p[:, cols].astype(F32) + r5m[:, cols].astype(F32)
-            outv[:, cols] = total.astype(BF16)
-        cols = chunk_cols(c)
-        store = pltpu.make_async_copy(outv.at[:, cols], out_hbm.at[:, cols], local_sem.at[4])
-        store.start()
+            out_ref[:, cols] = total.astype(BF16)
         stores.append(c)
 
     def drain_all(c=0):
@@ -527,10 +524,10 @@
         drain("meta", meta.at[pl.ds(0, 15)])
         for kind in ("rows", "back"):
             drain(kind, zsend.at[pl.ds(0, 11)])
-        for kind in ("near", "nearback"):
+        for kind in ("near", "nb"):
             drain(kind, frecv)
         drain("whole", fgath)
-        drain("mwhole", fmeta)
+        drain("mw", fmeta)
         drain("sum", fsum)
         drain("early", esend)
         for kind, like in (("1p", r1p), ("1m", r1m), ("4p", r4p), ("4m", r4m)):
@@ -551,7 +548,6 @@
     assert (len(leaving), len(landing)) == (LEAVING, LANDING), (len(leaving), len(landing))
     drain("5p", r5p)
     drain("5m", r5m)
-    pltpu.make_async_copy(outv, out_hbm, local_sem.at[4]).wait()
 
 
 def shards(n_hi, tokens, expert_ids, gate_probs, w_gate, w_up, w_down):
@@ -565,7 +561,7 @@
         functools.partial(kernel, (n_hi, tok, width, hid, most)),
         out_shape=jax.ShapeDtypeStruct((tok, width), BF16),
         in_specs=[hbm, vmem, hbm, hbm, hbm],
-        out_specs=hbm,
+        out_specs=vmem,
         scratch_shapes=[
             pltpu.VMEM((4, 4, tok, width), BF16),
             pltpu.VMEM((16, 8, 128), F32),
@@ -600,10 +596,9 @@
             pltpu.VMEM((tok // 2, width), BF16),
             pltpu.VMEM((tok, width), BF16),
             pltpu.VMEM((tok, width), BF16),
-            pltpu.VMEM((tok, width), BF16),
             pltpu.SemaphoreType.DMA((LEAVING,)),
             pltpu.SemaphoreType.DMA((LANDING,)),
-            pltpu.SemaphoreType.DMA((5,)),
+            pltpu.SemaphoreType.DMA((4,)),
         ],
         compiler_params=pltpu.CompilerParams(
             collective_id=0, has_side_effects=True, vmem_limit_bytes=54784 * 1024

time: 72 us -> 71.8 us (level)
  no operation moved by 1% of the time
where the time goes in v9:
time: 71.8 us; the launch traced here: 71.7 us
  Pallas kernels  70.3 us (98%)
    pallas_call x1, Pallas kernels, shards(): pl.pallas_call(functools.partial(kernel, (n_hi, tok, width, hid, most)),...  70.3 us

profile of v9, /device:TPU:1, one launch (start us, length us, event | category | flops | bytes accessed | tf_op | source)
XLA Modules:
  0.0 71.7 jit_solution(9814412808778676602)
XLA Ops:
  0.0 0.7 add_bitcast_fusion.routes_ref
  0.7 70.3 %routed_experts.1 = bf16[64,2048]{1,0:T(8,128)(2,1)S(1)} custom-call(bf16[64,2048]{1,0:T(8,128)(2,1)} %tok_hbm.1, f32[8,64]{1,0:T(8,128)S(1)} %add_bitcast_fusion.routes_ref, bf16[1,2048,768]{2,1,0:T(8,128)(2,1)} %wg_hbm.1, bf16[1,2048,768]{2,1,0:T(8,128)(2,1)} %wu_hbm.1, bf16[1,768,2048]{2,1,0:T(8,128)(2,1)} %wd_hbm.1), custom_call_target="tpu_custom_call" | custom-call | tf_op jit(solution)/shard_map/routed_experts/pallas_call | solution.py:560
  71.0 0.7 copy.8
